TPU v7x, 256 devices: a whole 4x4x8 slice. The times are simulated.
256 devices in a mesh: grid: 64 (over z, x, core), band: 4 (over y).
Axes of the slice: x: 4, y: 4, z: 8, core: 2. Of those that a mesh axis runs over, the one named last changes fastest.
Arguments:
- basis: float32 [2048, 65536], P('band', 'grid'), as said below
- panel: float32 [1024, 65536], P('band', 'grid'), may hold values from -6 to 6
Outputs:
- new_panel: float32 [1024, 65536], P('band', 'grid')
- coeffs: float32 [2048, 1024], P('band')
Inputs may be any that keep to these rules, and one draw needn't show every extreme that they name: The rows of basis are orthogonal to each other, each with squared sum 65536 (to float32 rounding).
All inputs are finite; a program needn't handle non-finite values.
Results may differ from a plain program's by a relative error of at most 0.000073.
Values sent between devices are 32-bit elements; how exact they have to be, the bound alone decides.
A program may use at most 128 MiB of HBM per device.

v0:
```python
import functools

import jax
import jax.numpy as jnp
from jax import lax
from jax.experimental import pallas as pl
from jax.experimental.pallas import tpu as pltpu
from jax.sharding import PartitionSpec as P

BLOCK = 128
ROWS = 8


def tdot(left, right):
    return lax.dot_general(
        left,
        right,
        (((1,), (1,)), ((), ())),
        precision=lax.Precision.HIGH,
        preferred_element_type=jnp.float32,
    )


def cdot(left, right):
    return lax.dot_general(
        left,
        right,
        (((0,), (0,)), ((), ())),
        precision=lax.Precision.HIGH,
        preferred_element_type=jnp.float32,
    )


def halves(x):
    high = x.astype(jnp.bfloat16)
    low = (x - high.astype(jnp.float32)).astype(jnp.bfloat16)
    return high, low


def left_parts(x):
    high, low = halves(x)
    return jnp.concatenate([high, high, low], 1)


def right_parts(x, axis):
    high, low = halves(x)
    return jnp.concatenate([high, low, high], axis)


def dot_nt(left, right):
    return lax.dot_general(
        left, right, (((1,), (1,)), ((), ())), preferred_element_type=jnp.float32
    )


def block_inverse(tiles):
    lanes = lax.broadcasted_iota(jnp.int32, (ROWS, BLOCK), 1)
    subs = lax.broadcasted_iota(jnp.int32, (ROWS, BLOCK), 0)
    shape = (ROWS, BLOCK)
    tiles = list(tiles)
    count = len(tiles)
    done = []
    for t in range(count):
        tile = tiles[t]
        base = ROWS * t
        here = (lanes >= base) & (lanes < base + ROWS)
        cols = [jnp.broadcast_to(tile[:, base + q : base + q + 1], shape) for q in range(ROWS)]
        entry = {
            (p, q): jnp.broadcast_to(cols[q][p : p + 1, :], shape)
            for q in range(ROWS)
            for p in range(q, ROWS)
        }
        start = jnp.where(here, jnp.where(lanes - base == subs, 1.0, 0.0), tile)
        rows = [jnp.broadcast_to(start[p : p + 1, :], shape) for p in range(ROWS)]
        unit = {}
        root = []
        scaled = []
        for q in range(ROWS):
            inv_root = lax.rsqrt(entry[q, q])
            inv = inv_root * inv_root
            root.append(inv_root)
            scaled.append(inv)
            for p in range(q + 1, ROWS):
                unit[p, q] = entry[p, q] * inv
            for p in range(q + 1, ROWS):
                for s in range(q + 1, p + 1):
                    entry[p, s] = entry[p, s] - unit[p, q] * entry[s, q]
                rows[p] = rows[p] - unit[p, q] * rows[q]
        out = rows[0] * root[0]
        for p in range(1, ROWS):
            out = jnp.where(subs == p, rows[p] * root[p], out)
        done.append(jnp.where(lanes <= base + subs, out, 0.0))
        if t + 1 < count:
            back = [rows[p] * scaled[p] for p in range(ROWS)]
            for p in range(ROWS - 1, 0, -1):
                for q in range(p):
                    back[q] = back[q] - unit[p, q] * back[p]
            for u in range(t + 1, count):
                old = tiles[u]
                new = jnp.where(here, 0.0, old)
                for p in range(ROWS):
                    new = new - jnp.broadcast_to(old[:, base + p : base + p + 1], shape) * back[p]
                tiles[u] = new
    return done


def factor_kernel(gram_ref, out_ref, diag_ref, right_ref):
    blocks = out_ref.shape[0] // BLOCK
    for pair in range(blocks // 2):
        rows = slice(pair * BLOCK, (pair + 1) * BLOCK)
        for row, tiles, first in ((pair, pair + 1, 0), (blocks - 1 - pair, blocks - pair, pair + 1)):
            for col in range(tiles):
                tile = gram_ref[rows, (first + col) * BLOCK : (first + col + 1) * BLOCK]
                out_ref[row * BLOCK : (row + 1) * BLOCK, col * BLOCK : (col + 1) * BLOCK] = tile
                if col < row:
                    out_ref[col * BLOCK : (col + 1) * BLOCK, row * BLOCK : (row + 1) * BLOCK] = tile.T

    def step(k, carry):
        at = pl.ds(pl.multiple_of(k * BLOCK, BLOCK), BLOCK)
        base = pl.multiple_of(k * BLOCK, BLOCK)
        tiles = [
            out_ref[pl.ds(base + ROWS * t, ROWS), at] for t in range(BLOCK // ROWS)
        ]
        for t, tile in enumerate(block_inverse(tiles)):
            diag_ref[pl.ds(ROWS * t, ROWS), :] = tile
        diag = diag_ref[...]
        panel = jnp.dot(
            left_parts(diag),
            right_parts(out_ref[at, :], 0),
            preferred_element_type=jnp.float32,
        )
        out_ref[at, :] = panel
        out_ref[at, at] = diag
        right_ref[...] = right_parts(out_ref[at, :], 0)
        diag_right = right_parts(diag, 1)

        def update(i, carry):
            rows = pl.ds(pl.multiple_of(i * BLOCK, BLOCK), BLOCK)
            lower = dot_nt(left_parts(out_ref[rows, at]), diag_right)
            out_ref[rows, at] = jnp.zeros((BLOCK, BLOCK), jnp.float32)
            out_ref[rows, :] -= jnp.dot(
                left_parts(lower), right_ref[...], preferred_element_type=jnp.float32
            )
            return carry

        lax.fori_loop(k + 1, blocks, update, 0)
        return carry

    lax.fori_loop(0, blocks, step, 0)
    row = lax.broadcasted_iota(jnp.int32, (BLOCK, out_ref.shape[1]), 0)
    col = lax.broadcasted_iota(jnp.int32, (BLOCK, out_ref.shape[1]), 1)

    def clear(i, carry):
        rows = pl.ds(pl.multiple_of(i * BLOCK, BLOCK), BLOCK)
        out_ref[rows, :] = jnp.where(col <= row + i * BLOCK, out_ref[rows, :], 0.0)
        return carry

    lax.fori_loop(0, blocks, clear, 0)


def inverse_factor(gram):
    n = 2 * gram.shape[0]
    return pl.pallas_call(
        factor_kernel,
        out_shape=jax.ShapeDtypeStruct((n, n), jnp.float32),
        in_specs=[pl.BlockSpec(memory_space=pltpu.VMEM)],
        out_specs=pl.BlockSpec(memory_space=pltpu.VMEM),
        scratch_shapes=[
            pltpu.VMEM((BLOCK, BLOCK), jnp.float32),
            pltpu.VMEM((3 * BLOCK, n), jnp.bfloat16),
        ],
        compiler_params=pltpu.CompilerParams(vmem_limit_bytes=32 * 1024 * 1024),
        cost_estimate=pl.CostEstimate(
            flops=60 * n * n * n, bytes_accessed=8 * n * n, transcendentals=n
        ),
    )(gram)


def pack(top, bottom, tiles):
    return jnp.concatenate([top[:, : tiles * BLOCK], bottom[:, : bottom.shape[1] + BLOCK - tiles * BLOCK]], 1)


def swap(x, band, bit):
    return lax.ppermute(x, "band", [(i, i ^ bit) for i in range(band)])


def body(basis, panel):
    grid, band = lax.axis_size("grid"), lax.axis_size("band")
    at_grid, at_band = lax.axis_index("grid"), lax.axis_index("band")
    n_grid = panel.shape[1] * grid
    rows_q = basis.shape[0]
    rows_p = panel.shape[0]
    n_panel = rows_p * band
    blocks = n_panel // BLOCK
    share_q, share_b = rows_q // grid, BLOCK // grid
    panel_all = lax.all_gather(panel, "band", axis=0, tiled=True)
    top = lax.dynamic_slice_in_dim(panel_all, at_band * BLOCK, BLOCK, 0)
    bottom = lax.dynamic_slice_in_dim(panel_all, (blocks - 1 - at_band) * BLOCK, BLOCK, 0)
    stacked = jnp.concatenate(
        [x.reshape(grid, x.shape[0] // grid, -1) for x in (basis, top, bottom)], 1
    ).reshape(rows_q + 2 * BLOCK, -1)
    both = tdot(stacked, panel_all)
    mine = lax.psum_scatter(both, "grid", scatter_dimension=0, tiled=True) / n_grid
    coeffs = lax.all_gather(mine[:share_q], "grid", axis=0, tiled=True)
    by_block = coeffs.reshape(rows_q, blocks, grid, share_b)
    picked = lax.dynamic_index_in_dim(by_block, at_grid, 2, keepdims=False)
    square = cdot(picked.reshape(rows_q, blocks * share_b), coeffs)
    square = square.reshape(blocks, share_b, n_panel)
    packed = jnp.concatenate(
        [pack(square[b], square[blocks - 1 - b], b + 1) for b in range(band)], 0
    )
    packed = lax.psum_scatter(packed, "band", scatter_dimension=0, tiled=True)
    mine_top = mine[share_q : share_q + share_b]
    mine_bottom = mine[share_q + share_b :]
    mine_packed = lax.switch(
        at_band, [functools.partial(pack, tiles=b + 1) for b in range(band)], mine_top, mine_bottom
    )
    gram = lax.all_gather(mine_packed - packed, ("band", "grid"), axis=0, tiled=True)

    bits = [1 << i for i in range(band.bit_length() - 1)]
    odd = at_band % 2

    def removed_rows(which):
        cols = [
            lax.dynamic_slice_in_dim(coeffs, (which + i) * rows_p, rows_p, 1)
            for i in range(0, band, 2)
        ]
        return cdot(jnp.concatenate(cols, 1), basis).reshape(band // 2, rows_p, -1)

    kept = removed_rows(odd) + swap(removed_rows(1 - odd), band, 1)
    for bit in bits[1:]:
        halves_of = kept.reshape(-1, 2, rows_p, kept.shape[-1])
        side = (at_band // bit) % 2
        sent = lax.dynamic_index_in_dim(halves_of, 1 - side, 1, keepdims=False)
        kept = lax.dynamic_index_in_dim(halves_of, side, 1, keepdims=False) + swap(sent, band, bit)
    projected = panel - kept.reshape(panel.shape)
    projected, gram = lax.optimization_barrier((projected, gram))
    others = [projected] + [swap(projected, band, d) for d in range(1, band)]
    inverse = inverse_factor(gram)
    inverse_rows = lax.dynamic_slice_in_dim(inverse, at_band * rows_p, rows_p, 0)
    new_panel = 0.0
    for d, rows in enumerate(others):
        cols = lax.dynamic_slice_in_dim(inverse_rows, (at_band ^ d) * rows_p, rows_p, 1)
        new_panel = new_panel + jnp.dot(cols, rows, precision=lax.Precision.HIGH)
    return (new_panel, coeffs)


def solution(mesh):
    placed = (P("band", "grid"), P("band", "grid"))
    return jax.shard_map(
        body,
        mesh=mesh,
        in_specs=placed,
        out_specs=(P("band", "grid"), P("band", None)),
        check_vma=False,
    )
```

profile of v0, /device:TPU:1, one launch (start us, length us, event | category | flops | bytes accessed | tf_op | source)
XLA Modules:
  0.0 494.3 jit_solution(13708234545750317090)
XLA Ops:
  8.0 56.3 %all-gather.5.cloned.1.call-done = f32[1024,1024]{1,0:T(8,128)} async-done(((f32[256,1024]{1,0:T(8,128)}), f32[1024,1024]{1,0:T(8,128)}) %all-gather.5.cloned.1.call-update) | async-done | bytes 4194320 | tf_op jit(solution)/shard_map/all_gather | solution.py:196
  64.2 2.1 constant_dynamic-slice_fusion.7
  68.0 2.6 pad_maximum_fusion.4
  70.5 3.0 reshape.57
  73.5 8.1 %fusion.20 = f32[768,1024]{1,0:T(8,128)} fusion(f32[768,1024]{1,0:T(8,128)S(1)} %reshape.57, f32[1024,1024]{1,0:T(8,128)} %all-gather.5.cloned.1.call-done), kind=kOutput, calls=%fused_computation.38 | convolution fusion | flops 4831838208 | bytes 10485760 | tf_op jit(solution)/shard_map/dot_general | solution.py:15
  81.6 70.6 %fusion = f32[16,1024]{1,0:T(8,128)S(1)} fusion(f32[768,1024]{1,0:T(8,128)} %fusion.20), kind=kCustom, calls=%all-reduce-scatter | all-reduce-scatter fusion | flops 1048577 | bytes 3212288
  154.2 4.0 collective-permute-start.10
  158.2 5.3 %collective-permute-start.11 = (f32[16,1024]{1,0:T(8,128)S(1)}, f32[16,1024]{1,0:T(8,128)S(1)}, u32[]{:S(2)}, u32[]{:S(2)}) collective-permute-start(f32[16,1024]{1,0:T(8,128)S(1)} %fusion), channel_id=1, source_target_pairs={{0,28},{4,32},{8,36},{12,40},{16,44},{20,48},{24,52},{28,56},{32,6... | collective-permute-start | bytes 196616
  163.6 3.1 collective-permute-start.12
  166.7 2.1 collective-permute-start.13
  168.8 2.6 collective-permute-start.14
  171.4 4.2 collective-permute-start.15
  175.6 3.5 collective-permute-start.16
  179.1 2.2 collective-permute-start.17
  181.3 2.5 collective-permute-start.18
  185.2 2.2 collective-permute-start.5
  187.4 2.2 collective-permute-start.6
  189.7 3.1 collective-permute-start.7
  192.7 3.1 collective-permute-start.8
  195.9 4.6 collective-permute-start.9
  202.3 2.2 concatenate.44
  206.7 73.9 %all-gather.7.cloned.1.call-done = f32[512,1024]{1,0:T(8,128)} async-done(((f32[8,1024]{1,0:T(8,128)}), f32[512,1024]{1,0:T(8,128)}) %all-gather.7.cloned.1.call-update) | async-done | bytes 2097168 | tf_op jit(solution)/shard_map/all_gather | solution.py:204
  280.6 2.9 copy.5
  283.5 3.6 reshape.61
  288.6 13.6 %all-reduce.1 = f32[8,1152]{1,0:T(8,128)S(1)} all-reduce(f32[8,1152]{1,0:T(8,128)S(1)} %maximum_maximum_fusion), channel_id=3, replica_groups=mesh['grid'=64,'band'=4] {'band'}, use_global_device_ids=true, to_apply=%region_5.6.clone | all-reduce | flops 9216 | bytes 73728
  304.4 3.3 fusion.6
  309.6 41.8 %collective-permute-done = f32[2,256,1024]{2,1,0:T(8,128)} collective-permute-done((f32[2,256,1024]{2,1,0:T(8,128)}, f32[2,256,1024]{2,1,0:T(8,128)}, u32[]{:S(2)}, u32[]{:S(2)}) %collective-permute-start) | collective-permute-done | bytes 2097184 | tf_op jit(solution)/shard_map/ppermute | solution.py:184
  351.4 2.0 add.94
  354.6 20.1 %collective-permute-done.1 = f32[1,256,1024]{2,1,0:T(8,128)} collective-permute-done((f32[1,256,1024]{2,1,0:T(8,128)S(1)}, f32[1,256,1024]{2,1,0:T(8,128)}, u32[]{:S(2)}, u32[]{:S(2)}) %collective-permute-start.1) | collective-permute-done | bytes 1048608 | tf_op jit(solution)/shard_map/ppermute | solution.py:184
  376.5 43.6 %all-gather.9.cloned.1.call-done = f32[256,2,1152]{2,1,0:T(2,128)} async-done(((f32[1,2,1152]{2,1,0:T(2,128)}), f32[256,2,1152]{2,1,0:T(2,128)}) %all-gather.9.cloned.1.call-update) | async-done | bytes 2359312 | tf_op jit(solution)/shard_map/all_gather | solution.py:218
  420.1 3.1 reshape.64.gram_ref
  426.9 55.9 %shard_map.41 = f32[1024,1024]{1,0:T(8,128)S(1)} custom-call(f32[512,1152]{1,0:T(8,128)S(1)} %reshape.64.gram_ref), custom_call_target="tpu_custom_call" | custom-call | flops 64424509440 | bytes 8388608 | tf_op jit(solution)/shard_map/pallas_call | solution.py:163
  (79 shorter events, 25.6 us)
Async XLA Ops:
  7.2 60.8 %copy-start.2 = (f32[512,1024]{1,0:T(8,128)S(1)}, f32[512,1024]{1,0:T(8,128)}, u32[]{:S(2)}) copy-start(f32[512,1024]{1,0:T(8,128)} %param.6) | copy-start | bytes 6291460
  7.2 57.1 %all-gather.5.cloned.1.call-start = ((), (), s32[]{:S(2)}) async-start(), calls=%async_computation | async-start | bytes 5242880 | tf_op jit(solution)/shard_map/all_gather | solution.py:196
  7.9 272.7 %all-gather.7.cloned.1.call-start = ((), (), s32[]{:S(2)}) async-start(), calls=%async_computation.1 | async-start | bytes 2129920 | tf_op jit(solution)/shard_map/all_gather | solution.py:204
  81.6 118.8 %copy-start.5 = (u32[256]{0:T(256)S(1)}, u32[256]{0:T(256)}, u32[]{:S(2)}) copy-start(u32[256]{0:T(256)} %constant.108) | copy-start | bytes 3076
  81.6 123.6 %copy-start.6 = (u32[256]{0:T(256)S(1)}, u32[256]{0:T(256)}, u32[]{:S(2)}) copy-start(u32[256]{0:T(256)} %constant.112) | copy-start | bytes 3076
  152.2 16.6 %collective-permute-start.20 = (f32[12,1024]{1,0:T(8,128)S(1)}, f32[12,1024]{1,0:T(8,128)S(1)}, u32[]{:S(2)}, u32[]{:S(2)}) collective-permute-start(f32[12,1024]{1,0:T(8,128)S(1)} %slice.98), channel_id=1, source_target_pairs={{0,64},{4,68},{8,72},{12,76},{16,80},{20,84},{24,88},{28,92},{32,9... | collective-permute-start | bytes 147464
  154.2 17.2 %collective-permute-start.10 = (f32[16,1024]{1,0:T(8,128)S(1)}, f32[16,1024]{1,0:T(8,128)S(1)}, u32[]{:S(2)}, u32[]{:S(2)}) collective-permute-start(f32[16,1024]{1,0:T(8,128)S(1)} %fusion), channel_id=1, source_target_pairs={{0,24},{4,28},{8,32},{12,36},{16,40},{20,44},{24,48},{28,52},{32,5... | collective-permute-start | bytes 196616
  158.2 17.4 %collective-permute-start.11 = (f32[16,1024]{1,0:T(8,128)S(1)}, f32[16,1024]{1,0:T(8,128)S(1)}, u32[]{:S(2)}, u32[]{:S(2)}) collective-permute-start(f32[16,1024]{1,0:T(8,128)S(1)} %fusion), channel_id=1, source_target_pairs={{0,28},{4,32},{8,36},{12,40},{16,44},{20,48},{24,52},{28,56},{32,6... | collective-permute-start | bytes 196616
  163.6 15.6 %collective-permute-start.12 = (f32[16,1024]{1,0:T(8,128)S(1)}, f32[16,1024]{1,0:T(8,128)S(1)}, u32[]{:S(2)}, u32[]{:S(2)}) collective-permute-start(f32[16,1024]{1,0:T(8,128)S(1)} %fusion), channel_id=1, source_target_pairs={{0,32},{4,36},{8,40},{12,44},{16,48},{20,52},{24,56},{28,60},{32,6... | collective-permute-start | bytes 196616
  166.7 14.6 %collective-permute-start.13 = (f32[16,1024]{1,0:T(8,128)S(1)}, f32[16,1024]{1,0:T(8,128)S(1)}, u32[]{:S(2)}, u32[]{:S(2)}) collective-permute-start(f32[16,1024]{1,0:T(8,128)S(1)} %fusion), channel_id=1, source_target_pairs={{0,36},{4,40},{8,44},{12,48},{16,52},{20,56},{24,60},{28,64},{32,6... | collective-permute-start | bytes 196616
  168.8 15.1 %collective-permute-start.14 = (f32[16,1024]{1,0:T(8,128)S(1)}, f32[16,1024]{1,0:T(8,128)S(1)}, u32[]{:S(2)}, u32[]{:S(2)}) collective-permute-start(f32[16,1024]{1,0:T(8,128)S(1)} %fusion), channel_id=1, source_target_pairs={{0,40},{4,44},{8,48},{12,52},{16,56},{20,60},{24,64},{28,68},{32,7... | collective-permute-start | bytes 196616
  171.4 13.8 %collective-permute-start.15 = (f32[16,1024]{1,0:T(8,128)S(1)}, f32[16,1024]{1,0:T(8,128)S(1)}, u32[]{:S(2)}, u32[]{:S(2)}) collective-permute-start(f32[16,1024]{1,0:T(8,128)S(1)} %fusion), channel_id=1, source_target_pairs={{0,44},{4,48},{8,52},{12,56},{16,60},{20,64},{24,68},{28,72},{32,7... | collective-permute-start | bytes 196616
  175.6 11.8 %collective-permute-start.16 = (f32[16,1024]{1,0:T(8,128)S(1)}, f32[16,1024]{1,0:T(8,128)S(1)}, u32[]{:S(2)}, u32[]{:S(2)}) collective-permute-start(f32[16,1024]{1,0:T(8,128)S(1)} %fusion), channel_id=1, source_target_pairs={{0,48},{4,52},{8,56},{12,60},{16,64},{20,68},{24,72},{28,76},{32,8... | collective-permute-start | bytes 196616
  179.1 10.5 %collective-permute-start.17 = (f32[16,1024]{1,0:T(8,128)S(1)}, f32[16,1024]{1,0:T(8,128)S(1)}, u32[]{:S(2)}, u32[]{:S(2)}) collective-permute-start(f32[16,1024]{1,0:T(8,128)S(1)} %fusion), channel_id=1, source_target_pairs={{0,52},{4,56},{8,60},{12,64},{16,68},{20,72},{24,76},{28,80},{32,8... | collective-permute-start | bytes 196616
  181.3 11.4 %collective-permute-start.18 = (f32[16,1024]{1,0:T(8,128)S(1)}, f32[16,1024]{1,0:T(8,128)S(1)}, u32[]{:S(2)}, u32[]{:S(2)}) collective-permute-start(f32[16,1024]{1,0:T(8,128)S(1)} %fusion), channel_id=1, source_target_pairs={{0,56},{4,60},{8,64},{12,68},{16,72},{20,76},{24,80},{28,84},{32,8... | collective-permute-start | bytes 196616
  183.9 12.0 %collective-permute-start.19 = (f32[16,1024]{1,0:T(8,128)S(1)}, f32[16,1024]{1,0:T(8,128)S(1)}, u32[]{:S(2)}, u32[]{:S(2)}) collective-permute-start(f32[16,1024]{1,0:T(8,128)S(1)} %fusion), channel_id=1, source_target_pairs={{0,60},{4,64},{8,68},{12,72},{16,76},{20,80},{24,84},{28,88},{32,9... | collective-permute-start | bytes 196616
  185.2 16.5 %collective-permute-start.5 = (f32[16,1024]{1,0:T(8,128)S(1)}, f32[16,1024]{1,0:T(8,128)S(1)}, u32[]{:S(2)}, u32[]{:S(2)}) collective-permute-start(f32[16,1024]{1,0:T(8,128)S(1)} %fusion), channel_id=1, source_target_pairs={{0,4},{4,8},{8,12},{12,16},{16,20},{20,24},{24,28},{28,32},{32,36}... | collective-permute-start | bytes 196616
  187.4 14.3 %collective-permute-start.6 = (f32[16,1024]{1,0:T(8,128)S(1)}, f32[16,1024]{1,0:T(8,128)S(1)}, u32[]{:S(2)}, u32[]{:S(2)}) collective-permute-start(f32[16,1024]{1,0:T(8,128)S(1)} %fusion), channel_id=1, source_target_pairs={{0,8},{4,12},{8,16},{12,20},{16,24},{20,28},{24,32},{28,36},{32,40... | collective-permute-start | bytes 196616
  189.7 12.0 %collective-permute-start.7 = (f32[16,1024]{1,0:T(8,128)S(1)}, f32[16,1024]{1,0:T(8,128)S(1)}, u32[]{:S(2)}, u32[]{:S(2)}) collective-permute-start(f32[16,1024]{1,0:T(8,128)S(1)} %fusion), channel_id=1, source_target_pairs={{0,12},{4,16},{8,20},{12,24},{16,28},{20,32},{24,36},{28,40},{32,4... | collective-permute-start | bytes 196616
  192.7 9.0 %collective-permute-start.8 = (f32[16,1024]{1,0:T(8,128)S(1)}, f32[16,1024]{1,0:T(8,128)S(1)}, u32[]{:S(2)}, u32[]{:S(2)}) collective-permute-start(f32[16,1024]{1,0:T(8,128)S(1)} %fusion), channel_id=1, source_target_pairs={{0,16},{4,20},{8,24},{12,28},{16,32},{20,36},{24,40},{28,44},{32,4... | collective-permute-start | bytes 196616
  195.9 6.5 %collective-permute-start.9 = (f32[16,1024]{1,0:T(8,128)S(1)}, f32[16,1024]{1,0:T(8,128)S(1)}, u32[]{:S(2)}, u32[]{:S(2)}) collective-permute-start(f32[16,1024]{1,0:T(8,128)S(1)} %fusion), channel_id=1, source_target_pairs={{0,20},{4,24},{8,28},{12,32},{16,36},{20,40},{24,44},{28,48},{32,5... | collective-permute-start | bytes 196616
  205.2 214.9 %all-gather.9.cloned.1.call-start = ((), (), s32[]{:S(2)}) async-start(), calls=%async_computation.2 | async-start | bytes 2368512 | tf_op jit(solution)/shard_map/all_gather | solution.py:218
  283.5 4.4 copy-start
  302.8 1.6 copy-start.3
  303.1 4.6 copy-start.4
  307.7 43.7 %collective-permute-start = (f32[2,256,1024]{2,1,0:T(8,128)}, f32[2,256,1024]{2,1,0:T(8,128)}, u32[]{:S(2)}, u32[]{:S(2)}) collective-permute-start(f32[2,256,1024]{2,1,0:T(8,128)} %bitcast.2), channel_id=1, source_target_pairs={{0,1},{1,0},{2,3},{3,2},{4,5},{5,4},{6,7},{7,6},{8,9},{9,8},{10,11... | collective-permute-start | bytes 6291464 | tf_op jit(solution)/shard_map/ppermute | solution.py:184
  353.5 21.2 %collective-permute-start.1 = (f32[1,256,1024]{2,1,0:T(8,128)S(1)}, f32[1,256,1024]{2,1,0:T(8,128)}, u32[]{:S(2)}, u32[]{:S(2)}) collective-permute-start(f32[1,256,1024]{2,1,0:T(8,128)S(1)} %constant_dynamic-slice_fusion.1), channel_id=1, source_target_pairs={{0,2},{1,3},{2,0},{3,1},{4,6},{5,7},{6,4},{7,5},{8,10},{9,11},{10,... | collective-permute-start | bytes 3145736 | tf_op jit(solution)/shard_map/ppermute | solution.py:184
  423.2 61.0 %collective-permute-start.2 = (f32[256,1024]{1,0:T(8,128)S(1)}, f32[256,1024]{1,0:T(8,128)S(1)}, u32[]{:S(2)}, u32[]{:S(2)}) collective-permute-start(f32[256,1024]{1,0:T(8,128)S(1)} %bitcast_subtract_fusion), channel_id=1, source_target_pairs={{0,1},{1,0},{2,3},{3,2},{4,5},{5,4},{6,7},{7,6},{8,9},{9,8},{10,11... | collective-permute-start | bytes 3145736 | tf_op jit(solution)/shard_map/ppermute | solution.py:184
  424.5 59.0 %collective-permute-start.4 = (f32[256,1024]{1,0:T(8,128)S(1)}, f32[256,1024]{1,0:T(8,128)S(1)}, u32[]{:S(2)}, u32[]{:S(2)}) collective-permute-start(f32[256,1024]{1,0:T(8,128)S(1)} %bitcast_subtract_fusion), channel_id=1, source_target_pairs={{0,3},{1,2},{2,1},{3,0},{4,7},{5,6},{6,5},{7,4},{8,11},{9,10},{10,... | collective-permute-start | bytes 3145736 | tf_op jit(solution)/shard_map/ppermute | solution.py:184
  426.3 58.5 %collective-permute-start.3 = (f32[256,1024]{1,0:T(8,128)S(1)}, f32[256,1024]{1,0:T(8,128)S(1)}, u32[]{:S(2)}, u32[]{:S(2)}) collective-permute-start(f32[256,1024]{1,0:T(8,128)S(1)} %bitcast_subtract_fusion), channel_id=1, source_target_pairs={{0,2},{1,3},{2,0},{3,1},{4,6},{5,7},{6,4},{7,5},{8,10},{9,11},{10,... | collective-permute-start | bytes 3145736 | tf_op jit(solution)/shard_map/ppermute | solution.py:184
  484.2 2.3 copy-start.1
Sparse Core Ops, SparseCore 0:
  9.8 54.3 all-gather.4
  205.3 75.2 all-gather.6
  302.9 117.1 all-gather.8
where the time goes:
time: 495 us; the launch traced here: 494 us
  waiting for transfers between devices  237 us (48%)
  blocking collectives  84.1 us (17%)
  Pallas kernels  55.9 us (11%)
  starting transfers between devices  52.9 us (11%)
  local copies, waits for them, and re-layouts  24.2 us (5%)
  matrix products  17.5 us (4%)
  between operations  15.7 us (3%)
  other arithmetic  7.01 us (1%)
    unnamed x2, blocking collectives  84.1 us
    all_gather x1, waiting for transfers between devices, body(): coeffs = lax.all_gather(mine[:share_q], 'grid', axis=0, tiled=True)  73.9 us
    ppermute x5, waiting for transfers between devices, swap(): return lax.ppermute(x, 'band', [(i, i ^ bit) for i in range(band)])  61.9 us
    all_gather x1, waiting for transfers between devices, body(): panel_all = lax.all_gather(panel, 'band', axis=0, tiled=True)  56.3 us
    pallas_call x1, Pallas kernels, inverse_factor(): pl.pallas_call(factor_kernel, out_shape=jax.ShapeDtypeStruct((n, n), jnp....  55.9 us
    unnamed x16, starting transfers between devices  48 us
    all_gather x1, waiting for transfers between devices, body(): lax.all_gather(mine_packed - packed, ('band', 'grid'), axis=0, tiled=True)  43.6 us
  transfers between devices with their start and end apart: 24, of which 6 were waited for; matrix products, arithmetic and copies ran while one was open for 3% of the time, Pallas kernels for 11%

commit v1 on v0

--- a/solution.py
+++ b/solution.py
@@ -9,16 +9,11 @@
 
 BLOCK = 128
 ROWS = 8
-
-
-def tdot(left, right):
-    return lax.dot_general(
-        left,
-        right,
-        (((1,), (1,)), ((), ())),
-        precision=lax.Precision.HIGH,
-        preferred_element_type=jnp.float32,
-    )
+CORES = 2
+BANDS = 4
+ROUNDS = 4
+ALONG_X = 4
+MESH = pl.DeviceIdType.MESH
 
 
 def cdot(left, right):
@@ -51,6 +46,380 @@
     return lax.dot_general(
         left, right, (((1,), (1,)), ((), ())), preferred_element_type=jnp.float32
     )
+
+
+def tile_of(band, core, turn):
+    one, two, three = (lax.rem(band + i, BANDS) for i in (1, 2, 3))
+    if turn == 0:
+        return 2 * band + core
+    if turn == 3:
+        return 2 * two + core
+    return 2 * (one + core * (three - one)) + turn - 1
+
+
+class Place:
+    def __init__(self, nx, nz):
+        self.nx, self.nz = nx, nz
+        self.grid = lax.axis_index("grid")
+        self.band = lax.axis_index("band")
+        self.core = lax.rem(self.grid, CORES)
+        self.x = lax.rem(lax.div(self.grid, CORES), nx)
+        self.z = lax.div(self.grid, CORES * nx)
+        self.at = self.x * nz + self.z
+
+    def id(self, z, x, core):
+        return {"grid": (z * self.nx + x) * CORES + core, "band": self.band}
+
+    def other_core(self):
+        return self.id(self.z, self.x, 1 - self.core)
+
+    def over_x(self):
+        for d in range(1, self.nx):
+            x = lax.rem(self.x + d, self.nx)
+            yield d - 1, x, self.id(self.z, x, self.core)
+
+    def over_z(self):
+        for d in range(1, self.nz):
+            z = lax.rem(self.z + d, self.nz)
+            yield d - 1, z, self.id(z, self.x, self.core)
+
+    def over_y(self):
+        for d in range(1, BANDS):
+            band = lax.rem(self.band + d, BANDS)
+            yield d - 1, band, {"grid": self.grid, "band": band}
+
+    def barrier(self):
+        sem = pltpu.get_barrier_semaphore()
+        ids = [self.other_core()]
+        ids += [i for _, _, i in self.over_x()]
+        ids += [i for _, _, i in self.over_z()]
+        ids += [i for _, _, i in self.over_y()]
+        for i in ids:
+            pl.semaphore_signal(sem, inc=1, device_id=i, device_id_type=MESH)
+        pl.semaphore_wait(sem, len(ids))
+
+
+def remote(src, dst, send, recv, device):
+    return pltpu.make_async_remote_copy(
+        src_ref=src,
+        dst_ref=dst,
+        send_sem=send,
+        recv_sem=recv,
+        device_id=device,
+        device_id_type=MESH,
+    )
+
+
+def await_bytes(ref, sem):
+    pltpu.make_async_copy(ref, ref, sem).wait()
+
+
+def reduce_kernel(
+    nx, nz, n_grid,
+    basis_ref, panel_ref,
+    coeffs_ref, own_ref,
+    others, lhs, rhs, part, from_core, from_x, from_z, gathered,
+    y_send, y_recv, send, recv,
+):
+    me = Place(nx, nz)
+    me.barrier()
+    nq, k = basis_ref.shape
+    np_ = panel_ref.shape[0]
+    pieces = nx * nz
+    rq, rp = nq // pieces, np_ // pieces
+    half = np_ // 2
+    lo, hi = pl.ds(0, half), pl.ds(half, half)
+    right = {"grid": me.grid, "band": lax.rem(me.band + 1, BANDS)}
+    left = {"grid": me.grid, "band": lax.rem(me.band + BANDS - 1, BANDS)}
+
+    def hop(i, src, dst, device):
+        return remote(src, dst, y_send.at[i], y_recv.at[i], device)
+
+    hops = [
+        hop(0, panel_ref.at[lo], others.at[2, lo], right),
+        hop(1, panel_ref.at[lo], others.at[0, lo], left),
+        hop(2, panel_ref.at[hi], others.at[2, hi], right),
+        hop(3, panel_ref.at[hi], others.at[0, hi], left),
+        hop(4, others.at[2, lo], others.at[1, lo], right),
+        hop(5, others.at[0, hi], others.at[1, hi], left),
+    ]
+    for h in hops[:4]:
+        h.start()
+
+    high, low = halves(basis_ref[...])
+    lhs[:nq, :k] = high
+    lhs[:nq, k : 2 * k] = high
+    lhs[:nq, 2 * k :] = low
+    high, low = halves(panel_ref[...])
+    lhs[nq:, :k] = high
+    lhs[nq:, k : 2 * k] = high
+    lhs[nq:, 2 * k :] = low
+
+    def multiply(q, tiles):
+        for t, tile in enumerate(tiles):
+            rows = slice(t * BLOCK, (t + 1) * BLOCK)
+            high, low = halves(tile)
+            rhs[rows, :k] = high
+            rhs[rows, k : 2 * k] = low
+            rhs[rows, 2 * k :] = high
+        out = dot_nt(lhs[:nq, :], rhs[...])
+        for t in range(2):
+            part[q, t, :, :rq, :] = out[:, t * BLOCK : (t + 1) * BLOCK].reshape(pieces, rq, BLOCK)
+        out = dot_nt(lhs[nq:, :], rhs[...])
+        for t in range(2):
+            part[q, t, :, rq:, :] = out[:, t * BLOCK : (t + 1) * BLOCK].reshape(pieces, rp, BLOCK)
+
+    mine_x = pl.ds(me.x * nz, nz)
+
+    def to_core(q):
+        remote(
+            part.at[q, 1 - me.core], from_core.at[q], send.at[0, q], recv.at[0, q], me.other_core()
+        ).start()
+
+    def to_x(q):
+        await_bytes(from_core.at[q], recv.at[0, q])
+        part[q, me.core] += from_core[q]
+        for d, x, device in me.over_x():
+            remote(
+                part.at[q, me.core, pl.ds(x * nz, nz)],
+                from_x.at[q, d],
+                send.at[1, q],
+                recv.at[1, q],
+                device,
+            ).start()
+
+    def to_z(q):
+        await_bytes(from_x.at[q], recv.at[1, q])
+        total = part[q, me.core, mine_x]
+        for d in range(nx - 1):
+            total = total + from_x[q, d]
+        part[q, me.core, mine_x] = total
+        for d, z, device in me.over_z():
+            remote(
+                part.at[q, me.core, me.x * nz + z],
+                from_z.at[q, d],
+                send.at[2, q],
+                recv.at[2, q],
+                device,
+            ).start()
+
+    def back_z(q):
+        await_bytes(from_z.at[q], recv.at[2, q])
+        total = part[q, me.core, me.at]
+        for d in range(nz - 1):
+            total = total + from_z[q, d]
+        total = total * (1.0 / n_grid)
+        own_ref[q] = total[rq:]
+        gathered[q, me.core, me.at] = total[:rq]
+        here = gathered.at[q, me.core, me.at]
+        for _, _, device in me.over_z():
+            remote(here, here, send.at[3, q], recv.at[3, q], device).start()
+
+    def back_x(q):
+        await_bytes(gathered.at[q, 0, pl.ds(0, nz - 1)], recv.at[3, q])
+        here = gathered.at[q, me.core, mine_x]
+        for _, _, device in me.over_x():
+            remote(here, here, send.at[4, q], recv.at[4, q], device).start()
+
+    def back_core(q):
+        await_bytes(gathered.at[q, 0, pl.ds(0, (nx - 1) * nz)], recv.at[4, q])
+        here = gathered.at[q, me.core]
+        remote(here, here, send.at[5, q], recv.at[5, q], me.other_core()).start()
+
+    def finish(q):
+        await_bytes(gathered.at[q, 0], recv.at[5, q])
+        for t in range(CORES):
+            at = pl.multiple_of(tile_of(me.band, t, q) * BLOCK, BLOCK)
+            coeffs_ref[:, pl.ds(at, BLOCK)] = gathered[q, t].reshape(nq, BLOCK)
+
+    multiply(0, (panel_ref[lo, :], panel_ref[hi, :]))
+    to_core(0)
+    to_x(0)
+    to_z(0)
+    hops[0].wait_recv()
+    hops[4].start()
+    hops[1].wait_recv()
+    multiply(1, (others[0, lo, :], others[2, lo, :]))
+    to_core(1)
+    back_z(0)
+    to_x(1)
+    back_x(0)
+    to_z(1)
+    hops[3].wait_recv()
+    hops[5].start()
+    hops[2].wait_recv()
+    multiply(2, (others[0, hi, :], others[2, hi, :]))
+    to_core(2)
+    back_z(1)
+    back_core(0)
+    to_x(2)
+    back_x(1)
+    to_z(2)
+    hops[4].wait_recv()
+    hops[5].wait_recv()
+    multiply(3, (others[1, lo, :], others[1, hi, :]))
+    to_core(3)
+    back_z(2)
+    to_x(3)
+    back_core(1)
+    back_x(2)
+    finish(0)
+    to_z(3)
+    back_core(2)
+    finish(1)
+    back_z(3)
+    finish(2)
+    back_x(3)
+    back_core(3)
+    for h in hops:
+        h.wait_send()
+    finish(3)
+    for q in range(ROUNDS):
+        await_bytes(from_core.at[q], send.at[0, q])
+        await_bytes(from_x.at[q], send.at[1, q])
+        await_bytes(from_z.at[q], send.at[2, q])
+        await_bytes(gathered.at[q, 0, pl.ds(0, nz - 1)], send.at[3, q])
+        await_bytes(gathered.at[q, 0, pl.ds(0, (nx - 1) * nz)], send.at[4, q])
+        await_bytes(gathered.at[q, 0], send.at[5, q])
+
+
+def reduce_products(nx, nz, n_grid, basis, panel):
+    nq, k = basis.shape
+    np_ = panel.shape[0]
+    pieces = nx * nz
+    rq, rp = nq // pieces, np_ // pieces
+    f32 = jnp.float32
+    return pl.pallas_call(
+        functools.partial(reduce_kernel, nx, nz, n_grid),
+        out_shape=(
+            jax.ShapeDtypeStruct((nq, np_ * BANDS), f32),
+            jax.ShapeDtypeStruct((ROUNDS, rp, BLOCK), f32),
+        ),
+        in_specs=[pl.BlockSpec(memory_space=pltpu.VMEM)] * 2,
+        out_specs=(pl.BlockSpec(memory_space=pltpu.VMEM),) * 2,
+        scratch_shapes=[
+            pltpu.VMEM((BANDS - 1, np_, k), f32),
+            pltpu.VMEM((nq + np_, 3 * k), jnp.bfloat16),
+            pltpu.VMEM((2 * BLOCK, 3 * k), jnp.bfloat16),
+            pltpu.VMEM((ROUNDS, CORES, pieces, rq + rp, BLOCK), f32),
+            pltpu.VMEM((ROUNDS, pieces, rq + rp, BLOCK), f32),
+            pltpu.VMEM((ROUNDS, nx - 1, nz, rq + rp, BLOCK), f32),
+            pltpu.VMEM((ROUNDS, nz - 1, rq + rp, BLOCK), f32),
+            pltpu.VMEM((ROUNDS, CORES, pieces, rq, BLOCK), f32),
+            pltpu.SemaphoreType.DMA((6,)),
+            pltpu.SemaphoreType.DMA((6,)),
+            pltpu.SemaphoreType.DMA((6, ROUNDS)),
+            pltpu.SemaphoreType.DMA((6, ROUNDS)),
+        ],
+        compiler_params=pltpu.CompilerParams(
+            collective_id=0, has_side_effects=True, vmem_limit_bytes=56 * 1024 * 1024
+        ),
+        cost_estimate=pl.CostEstimate(
+            flops=60 * 1024**3, bytes_accessed=8 * 1024 * 1024, transcendentals=0
+        ),
+    )(basis, panel)
+
+
+def gram_kernel(
+    nx, nz,
+    coeffs_ref, own_ref,
+    gram_ref,
+    rhs, square, to_y, from_y, gathered,
+    send, recv,
+):
+    me = Place(nx, nz)
+    me.barrier()
+    nq, n = coeffs_ref.shape
+    rp = own_ref.shape[1]
+    np_ = n // BANDS
+    count = BANDS * rp
+
+    high, low = halves(coeffs_ref[...])
+    rhs[:nq, :] = high
+    rhs[nq : 2 * nq, :] = low
+    rhs[2 * nq :, :] = high
+    row = lax.broadcasted_iota(jnp.int32, (count, n), 0)
+    col = lax.broadcasted_iota(jnp.int32, (count, n), 1)
+    want = lax.div(row, rp) * np_ + lax.rem(row, rp) + me.at * rp
+    pick = jnp.where(col == want, 1.0, 0.0).astype(jnp.bfloat16)
+    high = dot_nt(pick, rhs[:nq, :]).astype(jnp.bfloat16)
+    low = dot_nt(pick, rhs[nq : 2 * nq, :]).astype(jnp.bfloat16)
+    square[...] = jnp.dot(
+        jnp.concatenate([high, high, low], 1), rhs[...], preferred_element_type=jnp.float32
+    )
+    for band in range(BANDS):
+        for q in range(ROUNDS):
+            at = pl.multiple_of(tile_of(band, me.core, q) * BLOCK, BLOCK)
+            to_y[band, q] = square[band * rp : (band + 1) * rp, pl.ds(at, BLOCK)]
+    for d, band, device in me.over_y():
+        remote(to_y.at[band], from_y.at[d], send.at[0], recv.at[0], device).start()
+    total = own_ref[...] - to_y[me.band]
+    await_bytes(from_y, recv.at[0])
+    for d in range(BANDS - 1):
+        total = total - from_y[d]
+    here = gathered.at[me.core, me.x, me.z, me.band]
+    gathered[me.core, me.x, me.z, me.band] = total
+    for _, _, device in me.over_y():
+        remote(here, here, send.at[1], recv.at[1], device).start()
+    await_bytes(from_y, recv.at[1])
+    here = gathered.at[me.core, me.x, me.z]
+    for _, _, device in me.over_z():
+        remote(here, here, send.at[2], recv.at[2], device).start()
+    await_bytes(gathered.at[0, 0, pl.ds(0, nz - 1)], recv.at[2])
+    here = gathered.at[me.core, me.x]
+    for _, _, device in me.over_x():
+        remote(here, here, send.at[3], recv.at[3], device).start()
+    await_bytes(gathered.at[0, pl.ds(0, nx - 1)], recv.at[3])
+    here = gathered.at[me.core]
+    remote(here, here, send.at[4], recv.at[4], me.other_core()).start()
+    await_bytes(gathered.at[0], recv.at[4])
+    for band in range(BANDS):
+        for core in range(CORES):
+            for q in range(ROUNDS):
+                at = int(static_tile(band, core, q)) * BLOCK
+                gram_ref[band * np_ : (band + 1) * np_, at : at + BLOCK] = gathered[
+                    core, :, :, band, q
+                ].reshape(np_, BLOCK)
+    await_bytes(from_y, send.at[0])
+    await_bytes(from_y, send.at[1])
+    await_bytes(gathered.at[0, 0, pl.ds(0, nz - 1)], send.at[2])
+    await_bytes(gathered.at[0, pl.ds(0, nx - 1)], send.at[3])
+    await_bytes(gathered.at[0], send.at[4])
+
+
+def static_tile(band, core, turn):
+    if turn == 0:
+        return 2 * band + core
+    if turn == 3:
+        return 2 * ((band + 2) % BANDS) + core
+    return 2 * ((band + (3 if core else 1)) % BANDS) + turn - 1
+
+
+def gather_gram(nx, nz, coeffs, own):
+    nq, n = coeffs.shape
+    rp = own.shape[1]
+    f32 = jnp.float32
+    return pl.pallas_call(
+        functools.partial(gram_kernel, nx, nz),
+        out_shape=jax.ShapeDtypeStruct((n, n), f32),
+        in_specs=[pl.BlockSpec(memory_space=pltpu.VMEM)] * 2,
+        out_specs=pl.BlockSpec(memory_space=pltpu.VMEM),
+        scratch_shapes=[
+            pltpu.VMEM((3 * nq, n), jnp.bfloat16),
+            pltpu.VMEM((BANDS * rp, n), f32),
+            pltpu.VMEM((BANDS, ROUNDS, rp, BLOCK), f32),
+            pltpu.VMEM((BANDS - 1, ROUNDS, rp, BLOCK), f32),
+            pltpu.VMEM((CORES, nx, nz, BANDS, ROUNDS, rp, BLOCK), f32),
+            pltpu.SemaphoreType.DMA((5,)),
+            pltpu.SemaphoreType.DMA((5,)),
+        ],
+        compiler_params=pltpu.CompilerParams(
+            collective_id=1, has_side_effects=True, vmem_limit_bytes=40 * 1024 * 1024
+        ),
+        cost_estimate=pl.CostEstimate(
+            flops=40 * 1024**3, bytes_accessed=8 * 1024 * 1024, transcendentals=0
+        ),
+    )(coeffs, own)
 
 
 def block_inverse(tiles):
@@ -106,14 +475,7 @@
 
 def factor_kernel(gram_ref, out_ref, diag_ref, right_ref):
     blocks = out_ref.shape[0] // BLOCK
-    for pair in range(blocks // 2):
-        rows = slice(pair * BLOCK, (pair + 1) * BLOCK)
-        for row, tiles, first in ((pair, pair + 1, 0), (blocks - 1 - pair, blocks - pair, pair + 1)):
-            for col in range(tiles):
-                tile = gram_ref[rows, (first + col) * BLOCK : (first + col + 1) * BLOCK]
-                out_ref[row * BLOCK : (row + 1) * BLOCK, col * BLOCK : (col + 1) * BLOCK] = tile
-                if col < row:
-                    out_ref[col * BLOCK : (col + 1) * BLOCK, row * BLOCK : (row + 1) * BLOCK] = tile.T
+    out_ref[...] = gram_ref[...]
 
     def step(k, carry):
         at = pl.ds(pl.multiple_of(k * BLOCK, BLOCK), BLOCK)
@@ -159,7 +521,7 @@
 
 
 def inverse_factor(gram):
-    n = 2 * gram.shape[0]
+    n = gram.shape[0]
     return pl.pallas_call(
         factor_kernel,
         out_shape=jax.ShapeDtypeStruct((n, n), jnp.float32),
@@ -176,46 +538,18 @@
     )(gram)
 
 
-def pack(top, bottom, tiles):
-    return jnp.concatenate([top[:, : tiles * BLOCK], bottom[:, : bottom.shape[1] + BLOCK - tiles * BLOCK]], 1)
-
-
 def swap(x, band, bit):
     return lax.ppermute(x, "band", [(i, i ^ bit) for i in range(band)])
 
 
 def body(basis, panel):
     grid, band = lax.axis_size("grid"), lax.axis_size("band")
-    at_grid, at_band = lax.axis_index("grid"), lax.axis_index("band")
+    at_band = lax.axis_index("band")
     n_grid = panel.shape[1] * grid
-    rows_q = basis.shape[0]
     rows_p = panel.shape[0]
-    n_panel = rows_p * band
-    blocks = n_panel // BLOCK
-    share_q, share_b = rows_q // grid, BLOCK // grid
-    panel_all = lax.all_gather(panel, "band", axis=0, tiled=True)
-    top = lax.dynamic_slice_in_dim(panel_all, at_band * BLOCK, BLOCK, 0)
-    bottom = lax.dynamic_slice_in_dim(panel_all, (blocks - 1 - at_band) * BLOCK, BLOCK, 0)
-    stacked = jnp.concatenate(
-        [x.reshape(grid, x.shape[0] // grid, -1) for x in (basis, top, bottom)], 1
-    ).reshape(rows_q + 2 * BLOCK, -1)
-    both = tdot(stacked, panel_all)
-    mine = lax.psum_scatter(both, "grid", scatter_dimension=0, tiled=True) / n_grid
-    coeffs = lax.all_gather(mine[:share_q], "grid", axis=0, tiled=True)
-    by_block = coeffs.reshape(rows_q, blocks, grid, share_b)
-    picked = lax.dynamic_index_in_dim(by_block, at_grid, 2, keepdims=False)
-    square = cdot(picked.reshape(rows_q, blocks * share_b), coeffs)
-    square = square.reshape(blocks, share_b, n_panel)
-    packed = jnp.concatenate(
-        [pack(square[b], square[blocks - 1 - b], b + 1) for b in range(band)], 0
-    )
-    packed = lax.psum_scatter(packed, "band", scatter_dimension=0, tiled=True)
-    mine_top = mine[share_q : share_q + share_b]
-    mine_bottom = mine[share_q + share_b :]
-    mine_packed = lax.switch(
-        at_band, [functools.partial(pack, tiles=b + 1) for b in range(band)], mine_top, mine_bottom
-    )
-    gram = lax.all_gather(mine_packed - packed, ("band", "grid"), axis=0, tiled=True)
+    nz = grid // (CORES * ALONG_X)
+    coeffs, own = reduce_products(ALONG_X, nz, n_grid, basis, panel)
+    gram = gather_gram(ALONG_X, nz, coeffs, own)
 
     bits = [1 << i for i in range(band.bit_length() - 1)]
     odd = at_band % 2

time: 495 us -> 277 us (0.56)
  waiting for transfers between devices: 237 us -> 45.6 us
  Pallas kernels: 55.9 us -> 206 us
  blocking collectives: 84.1 us -> 0 us
  starting transfers between devices: 52.9 us -> 4.04 us
  local copies, waits for them, and re-layouts: 24.2 us -> 7.52 us
  between operations: 15.7 us -> 0.79 us
  matrix products: 17.5 us -> 8.72 us
    all_gather x3 -> x0, waiting for transfers between devices: 174 us -> none  [the longest x1 73.9 us: body(): coeffs = lax.all_gather(mine[:share_q], 'grid', axis=0, tiled=True)]
    pallas_call x0 -> x2, Pallas kernels: none -> 150 us  [the longest x1 80 us: reduce_products(): pl.pallas_call(functools.partial(reduce_kernel, nx, nz, n_grid), out_shap...]
    unnamed x2 -> x0, blocking collectives: 84.1 us -> none
    unnamed x16 -> x0, starting transfers between devices: 48 us -> none
    ppermute x5, waiting for transfers between devices: 61.9 us -> 45.6 us  [swap(): return lax.ppermute(x, 'band', [(i, i ^ bit) for i in range(band)])]
    reshape x5 -> x0, local copies, waits for them, and re-layouts: 8.25 us -> none  [the longest x1 3.58 us: body(): by_block = coeffs.reshape(rows_q, blocks, grid, share_b)]
    dot_general x1 -> x0, matrix products: 8.09 us -> none  [tdot(): lax.dot_general(left, right, (((1,), (1,)), ((), ())), precision=lax.Prec...]
  transfers between devices with their start and end apart: 24 -> 5, of which waited for: 6 -> 1; matrix products, arithmetic and copies ran while one was open for 3% -> 1% of each run, Pallas kernels for 11% -> 46%
where the time goes in v1:
time: 277 us
  Pallas kernels  206 us (74%)
  waiting for transfers between devices  45.6 us (16%)
  matrix products  8.72 us (3%)
  local copies, waits for them, and re-layouts  7.52 us (3%)
  starting transfers between devices  4.04 us (1%)
  other arithmetic  3.96 us (1%)
    pallas_call x1, Pallas kernels, reduce_products(): pl.pallas_call(functools.partial(reduce_kernel, nx, nz, n_grid), out_shap...  80 us
    pallas_call x1, Pallas kernels, gather_gram(): pl.pallas_call(functools.partial(gram_kernel, nx, nz), out_shape=jax.Shap...  70.3 us
    pallas_call x1, Pallas kernels, inverse_factor(): pl.pallas_call(factor_kernel, out_shape=jax.ShapeDtypeStruct((n, n), jnp....  55.7 us
    ppermute x5, waiting for transfers between devices, swap(): return lax.ppermute(x, 'band', [(i, i ^ bit) for i in range(band)])  45.6 us
  transfers between devices with their start and end apart: 5, of which 1 were waited for; matrix products, arithmetic and copies ran while one was open for 1% of the time, Pallas kernels for 46%

profile of v1, /device:TPU:1, one launch (start us, length us, event | category | flops | bytes accessed | tf_op | source)
XLA Modules:
  0.0 276.5 jit_solution(5915938236484827667)
XLA Ops:
  0.7 80.0 %shard_map.41 = (f32[512,1024]{1,0:T(8,128)}, f32[4,8,128]{2,1,0:T(8,128)}) custom-call(f32[512,1024]{1,0:T(8,128)} %basis_ref.1, f32[256,1024]{1,0:T(8,128)} %panel_ref.1), custom_call_target="tpu_custom_call" | custom-call | flops 64424509440 | bytes 8388608 | tf_op jit(solution)/shard_map/pallas_call | solution.py:292
  80.6 0.0 copy-start.5
  80.7 1.8 constant_dynamic-slice_fusion.2
  82.5 0.4 copy-done.5
  82.9 3.2 %fusion.5 = f32[512,1024]{1,0:T(8,128)} fusion(f32[512,1024]{1,0:T(8,128)S(1)} %copy-done.5, f32[512,256]{1,0:T(8,128)S(1)} %get-tuple-element.11, f32[512,256]{1,0:T(8,128)S(1)} %get-tuple-element.10), kind=kOutput, calls=%fused_computation.7 | convolution fusion | flops 1610874880 | bytes 5242880 | tf_op jit(solution)/shard_map/dot_general | solution.py:20
  86.1 0.0 collective-permute-start
  86.1 1.9 fusion.1
  88.0 45.6 %collective-permute-done = f32[2,256,1024]{2,1,0:T(8,128)} collective-permute-done((f32[2,256,1024]{2,1,0:T(8,128)}, f32[2,256,1024]{2,1,0:T(8,128)}, u32[]{:S(2)}, u32[]{:S(2)}) %collective-permute-start) | collective-permute-done | bytes 2097184 | tf_op jit(solution)/shard_map/ppermute | solution.py:542
  133.6 2.0 add.78
  135.6 0.0 copy-start.4
  135.6 0.0 copy-start
  135.6 1.0 constant_dynamic-slice_fusion
  136.7 0.7 collective-permute-start.1
  137.4 0.0 copy-done.3
  137.4 1.0 copy-done
  138.3 70.3 %shard_map.42.gram_ref = f32[1024,1024]{1,0:T(8,128)S(1)} custom-call(f32[512,1024]{1,0:T(8,128)S(1)} %copy-done, f32[4,8,128]{2,1,0:T(8,128)S(1)} %copy-done.3), custom_call_target="tpu_custom_call" | custom-call | flops 42949672960 | bytes 8388608 | tf_op jit(solution)/shard_map/pallas_call | solution.py:402
  208.6 1.9 copy-done.1
  210.5 0.0 collective-permute-done.1
  210.5 0.0 copy-done.6
  210.6 2.0 bitcast_subtract_fusion
  212.5 0.7 collective-permute-start.2
  213.2 1.7 collective-permute-start.4
  214.9 1.0 collective-permute-start.3
  215.9 55.7 %shard_map.43 = f32[1024,1024]{1,0:T(8,128)S(1)} custom-call(f32[1024,1024]{1,0:T(8,128)S(1)} %copy-done.2), custom_call_target="tpu_custom_call" | custom-call | flops 64424509440 | bytes 8388608 | tf_op jit(solution)/shard_map/pallas_call | solution.py:525
  271.5 0.6 fusion.13
  272.2 0.0 collective-permute-done.4
  272.2 0.6 fusion.9
  272.9 0.0 collective-permute-done.2
  272.9 0.7 convolution_add_fusion.1
  273.5 0.0 collective-permute-done.3
  273.5 1.6 fusion
  275.2 1.3 copy.5
  (6 shorter events, 0.0 us)
Async XLA Ops:
  80.6 2.2 copy-start.5
  86.1 47.5 %collective-permute-start = (f32[2,256,1024]{2,1,0:T(8,128)}, f32[2,256,1024]{2,1,0:T(8,128)}, u32[]{:S(2)}, u32[]{:S(2)}) collective-permute-start(f32[2,256,1024]{2,1,0:T(8,128)} %bitcast.1), channel_id=1, source_target_pairs={{0,1},{1,0},{2,3},{3,2},{4,5},{5,4},{6,7},{7,6},{8,9},{9,8},{10,11... | collective-permute-start | bytes 6291464 | tf_op jit(solution)/shard_map/ppermute | solution.py:542
  133.6 3.8 %copy-start.3 = (f32[4,8,128]{2,1,0:T(8,128)S(1)}, f32[4,8,128]{2,1,0:T(8,128)}, u32[]{:S(2)}) copy-start(f32[4,8,128]{2,1,0:T(8,128)} %get-tuple-element.7.own_ref) | copy-start | bytes 49156
  135.6 1.8 copy-start.4
  135.6 2.7 copy-start
  136.7 73.9 %collective-permute-start.1 = (f32[1,256,1024]{2,1,0:T(8,128)}, f32[1,256,1024]{2,1,0:T(8,128)}, u32[]{:S(2)}, u32[]{:S(2)}) collective-permute-start(f32[1,256,1024]{2,1,0:T(8,128)} %constant_dynamic-slice_fusion), channel_id=1, source_target_pairs={{0,2},{1,3},{2,0},{3,1},{4,6},{5,7},{6,4},{7,5},{8,10},{9,11},{10,... | collective-permute-start | bytes 3145736 | tf_op jit(solution)/shard_map/ppermute | solution.py:542
  138.3 72.2 %copy-start.6 = (f32[256,1024]{1,0:T(8,128)S(1)}, f32[256,1024]{1,0:T(8,128)}, u32[]{:S(2)}) copy-start(f32[256,1024]{1,0:T(8,128)} %panel_ref.1) | copy-start | bytes 3145732
  208.6 1.9 copy-start.1
  210.5 5.3 %copy-start.2 = (f32[1024,1024]{1,0:T(8,128)S(1)}, f32[1024,1024]{1,0:T(8,128)}, u32[]{:S(2)}) copy-start(f32[1024,1024]{1,0:T(8,128)} %copy-done.1) | copy-start | bytes 12582916
  212.5 60.3 %collective-permute-start.2 = (f32[256,1024]{1,0:T(8,128)S(1)}, f32[256,1024]{1,0:T(8,128)S(1)}, u32[]{:S(2)}, u32[]{:S(2)}) collective-permute-start(f32[256,1024]{1,0:T(8,128)S(1)} %bitcast_subtract_fusion), channel_id=1, source_target_pairs={{0,1},{1,0},{2,3},{3,2},{4,5},{5,4},{6,7},{7,6},{8,9},{9,8},{10,11... | collective-permute-start | bytes 3145736 | tf_op jit(solution)/shard_map/ppermute | solution.py:542
  213.2 59.0 %collective-permute-start.4 = (f32[256,1024]{1,0:T(8,128)S(1)}, f32[256,1024]{1,0:T(8,128)S(1)}, u32[]{:S(2)}, u32[]{:S(2)}) collective-permute-start(f32[256,1024]{1,0:T(8,128)S(1)} %bitcast_subtract_fusion), channel_id=1, source_target_pairs={{0,3},{1,2},{2,1},{3,0},{4,7},{5,6},{6,5},{7,4},{8,11},{9,10},{10,... | collective-permute-start | bytes 3145736 | tf_op jit(solution)/shard_map/ppermute | solution.py:542
  214.9 58.6 %collective-permute-start.3 = (f32[256,1024]{1,0:T(8,128)S(1)}, f32[256,1024]{1,0:T(8,128)S(1)}, u32[]{:S(2)}, u32[]{:S(2)}) collective-permute-start(f32[256,1024]{1,0:T(8,128)S(1)} %bitcast_subtract_fusion), channel_id=1, source_target_pairs={{0,2},{1,3},{2,0},{3,1},{4,6},{5,7},{6,4},{7,5},{8,10},{9,11},{10,... | collective-permute-start | bytes 3145736 | tf_op jit(solution)/shard_map/ppermute | solution.py:542

commit v2 on v1

--- a/solution.py
+++ b/solution.py
@@ -12,18 +12,9 @@
 CORES = 2
 BANDS = 4
 ROUNDS = 4
+KEPT = 3
 ALONG_X = 4
 MESH = pl.DeviceIdType.MESH
-
-
-def cdot(left, right):
-    return lax.dot_general(
-        left,
-        right,
-        (((0,), (0,)), ((), ())),
-        precision=lax.Precision.HIGH,
-        preferred_element_type=jnp.float32,
-    )
 
 
 def halves(x):
@@ -52,9 +43,11 @@
     one, two, three = (lax.rem(band + i, BANDS) for i in (1, 2, 3))
     if turn == 0:
         return 2 * band + core
-    if turn == 3:
-        return 2 * two + core
-    return 2 * (one + core * (three - one)) + turn - 1
+    if turn == 1:
+        return 2 * (one + core * (three - one))
+    if turn == 2:
+        return 2 * (three + core * (one - three)) + 1
+    return 2 * two + core
 
 
 class Place:
@@ -114,12 +107,13 @@
     pltpu.make_async_copy(ref, ref, sem).wait()
 
 
-def reduce_kernel(
+def gather_kernel(
     nx, nz, n_grid,
     basis_ref, panel_ref,
-    coeffs_ref, own_ref,
-    others, lhs, rhs, part, from_core, from_x, from_z, gathered,
-    y_send, y_recv, send, recv,
+    coeffs_ref, gram_ref, projected_ref,
+    others, lhs, rhs, part, from_core, from_x, from_z, gathered, own,
+    removed, from_band, stacked, share, pieces_of,
+    y_send, y_recv, send, recv, b_send, b_recv, g_send, z_recv, x_recv, g_recv,
 ):
     me = Place(nx, nz)
     me.barrier()
@@ -209,7 +203,7 @@
         for d in range(nz - 1):
             total = total + from_z[q, d]
         total = total * (1.0 / n_grid)
-        own_ref[q] = total[rq:]
+        own[q] = total[rq:]
         gathered[q, me.core, me.at] = total[:rq]
         here = gathered.at[q, me.core, me.at]
         for _, _, device in me.over_z():
@@ -231,6 +225,28 @@
         for t in range(CORES):
             at = pl.multiple_of(tile_of(me.band, t, q) * BLOCK, BLOCK)
             coeffs_ref[:, pl.ds(at, BLOCK)] = gathered[q, t].reshape(nq, BLOCK)
+
+    def remove(q):
+        parts = [halves(gathered[q, t].reshape(nq, BLOCK).T) for t in range(CORES)]
+        high = jnp.concatenate([p[0] for p in parts], 0)
+        both = jnp.concatenate([high] + [p[1] for p in parts], 0)
+        out = jnp.dot(both, lhs[:nq, :k], preferred_element_type=jnp.float32)
+        out = out[: 2 * BLOCK] + out[2 * BLOCK :]
+        out = out + jnp.dot(high, lhs[:nq, 2 * k :], preferred_element_type=jnp.float32)
+        removed[q] = out.reshape(CORES, BLOCK, k)
+
+    across = {"grid": me.grid, "band": lax.rem(me.band + 2, BANDS)}
+
+    def bulk(i, src, dst, device):
+        return remote(src, dst, b_send.at[i], b_recv.at[i], device)
+
+    bulks = [
+        bulk(0, removed.at[1, 0], from_band.at[0, 0], right),
+        bulk(1, removed.at[1, 1], from_band.at[2, 0], left),
+        bulk(2, removed.at[2, 0], from_band.at[2, 1], left),
+        bulk(3, removed.at[2, 1], from_band.at[0, 1], right),
+        bulk(4, removed.at[3], from_band.at[1], across),
+    ]
 
     multiply(0, (panel_ref[lo, :], panel_ref[hi, :]))
     to_core(0)
@@ -248,7 +264,7 @@
     hops[3].wait_recv()
     hops[5].start()
     hops[2].wait_recv()
-    multiply(2, (others[0, hi, :], others[2, hi, :]))
+    multiply(2, (others[2, hi, :], others[0, hi, :]))
     to_core(2)
     back_z(1)
     back_core(0)
@@ -267,13 +283,114 @@
     to_z(3)
     back_core(2)
     finish(1)
+    remove(1)
+    bulks[0].start()
+    bulks[1].start()
     back_z(3)
     finish(2)
+    remove(2)
     back_x(3)
+    remove(0)
     back_core(3)
     for h in hops:
         h.wait_send()
     finish(3)
+
+    high, low = halves(coeffs_ref[...])
+    stacked[:nq, :] = high
+    stacked[nq : 2 * nq, :] = low
+    stacked[2 * nq :, :] = high
+    n = coeffs_ref.shape[1]
+    count = BANDS * rp
+    row = lax.broadcasted_iota(jnp.int32, (count, n), 0)
+    col = lax.broadcasted_iota(jnp.int32, (count, n), 1)
+    want = lax.div(row, rp) * np_ + lax.rem(row, rp) + me.at * rp
+    pick = jnp.where(col == want, 1.0, 0.0).astype(jnp.bfloat16)
+    high = dot_nt(pick, stacked[:nq, :]).astype(jnp.bfloat16)
+    low = dot_nt(pick, stacked[nq : 2 * nq, :]).astype(jnp.bfloat16)
+    square = jnp.dot(
+        jnp.concatenate([high, high, low], 1), stacked[...], preferred_element_type=jnp.float32
+    )
+    for band in range(BANDS):
+        rows = square[band * rp : (band + 1) * rp]
+        for i in range(KEPT):
+            first = 2 * ((band + i) % BANDS) * BLOCK
+            pair = [rows[:, first + t * BLOCK : first + (t + 1) * BLOCK] for t in range(CORES)]
+            share[me.band, band, i] = -jnp.where(me.core == 0, pair[0], pair[1])
+    for i, q in enumerate((0, 1 + me.core, ROUNDS - 1)):
+        share[me.band, me.band, i] += own[q]
+    for _, _, device in me.over_y():
+        remote(share.at[me.band], share.at[me.band], g_send.at[0], g_recv.at[0], device).start()
+    bulks[2].start()
+    bulks[3].start()
+    remove(3)
+    bulks[4].start()
+    await_bytes(share.at[pl.ds(0, BANDS - 1)], g_recv.at[0])
+    pieces_of[me.core, me.x, me.z] = (share[0] + share[1]) + (share[2] + share[3])
+
+    up, down = lax.rem(me.x + 1, nx), lax.rem(me.x + nx - 1, nx)
+    to_up, to_down = me.id(me.z, up, me.core), me.id(me.z, down, me.core)
+    first, second = pl.ds(0, BANDS // 2), pl.ds(BANDS // 2, BANDS // 2)
+
+    def spread(i, z):
+        here = pieces_of.at[me.core, me.x, z]
+        remote(here, here, g_send.at[2], x_recv.at[0, i], to_up).start()
+        remote(here, here, g_send.at[2], x_recv.at[1, i], to_down).start()
+
+    def relay(i, z):
+        await_bytes(pieces_of.at[0, 0, 0], x_recv.at[0, i])
+        here = pieces_of.at[me.core, down, z, first]
+        remote(here, here, g_send.at[3], g_recv.at[1], to_up).start()
+        await_bytes(pieces_of.at[0, 0, 0], x_recv.at[1, i])
+        here = pieces_of.at[me.core, up, z, second]
+        remote(here, here, g_send.at[3], g_recv.at[1], to_down).start()
+
+    def cross(x):
+        here = pieces_of.at[me.core, x]
+        remote(here, here, g_send.at[4], g_recv.at[2], me.other_core()).start()
+
+    here = pieces_of.at[me.core, me.x, me.z]
+    for d, _, device in me.over_z():
+        remote(here, here, g_send.at[1], z_recv.at[d], device).start()
+    spread(0, me.z)
+    order = [me.z]
+    for i, d in enumerate(sorted(range(1, nz), key=lambda d: min(d, nz - d))):
+        z = lax.rem(me.z + nz - d, nz)
+        await_bytes(pieces_of.at[0, 0, 0], z_recv.at[d - 1])
+        spread(i + 1, z)
+        relay(i, order[i])
+        order.append(z)
+    cross(me.x)
+    relay(nz - 1, order[nz - 1])
+    cross(up)
+    cross(down)
+    await_bytes(pieces_of.at[0, 0], g_recv.at[1])
+    cross(lax.rem(me.x + 2, nx))
+
+    def place(core):
+        for band in range(BANDS):
+            for i in range(KEPT):
+                at = (2 * ((band + i) % BANDS) + core) * BLOCK
+                tile = pieces_of[core, :, :, band, i].reshape(np_, BLOCK)
+                gram_ref[band * np_ : (band + 1) * np_, at : at + BLOCK] = tile
+                if i == 1:
+                    to = (2 * ((band + i) % BANDS) + core) * BLOCK
+                    gram_ref[to : to + BLOCK, band * np_ : (band + 1) * np_] = tile.T
+
+    await_bytes(pieces_of.at[0], g_recv.at[2])
+    place(0)
+    place(1)
+    for h in bulks:
+        h.wait_recv()
+    for t in range(CORES):
+        rows = slice(t * BLOCK, (t + 1) * BLOCK)
+        total = removed[0, t]
+        for d in range(BANDS - 1):
+            total = total + from_band[d, t]
+        projected_ref[rows, :] = panel_ref[rows, :] - total
+
+    for h in bulks:
+        h.wait_send()
     for q in range(ROUNDS):
         await_bytes(from_core.at[q], send.at[0, q])
         await_bytes(from_x.at[q], send.at[1, q])
@@ -281,22 +398,30 @@
         await_bytes(gathered.at[q, 0, pl.ds(0, nz - 1)], send.at[3, q])
         await_bytes(gathered.at[q, 0, pl.ds(0, (nx - 1) * nz)], send.at[4, q])
         await_bytes(gathered.at[q, 0], send.at[5, q])
-
-
-def reduce_products(nx, nz, n_grid, basis, panel):
+    await_bytes(share.at[pl.ds(0, BANDS - 1)], g_send.at[0])
+    await_bytes(pieces_of.at[0, 0, pl.ds(0, nz - 1)], g_send.at[1])
+    await_bytes(pieces_of.at[0, pl.ds(0, 2)], g_send.at[2])
+    await_bytes(pieces_of.at[0, 0], g_send.at[3])
+    await_bytes(pieces_of.at[0], g_send.at[4])
+
+
+def reduce_and_project(nx, nz, n_grid, basis, panel):
     nq, k = basis.shape
     np_ = panel.shape[0]
+    n = np_ * BANDS
     pieces = nx * nz
     rq, rp = nq // pieces, np_ // pieces
     f32 = jnp.float32
+    dma = pltpu.SemaphoreType.DMA
     return pl.pallas_call(
-        functools.partial(reduce_kernel, nx, nz, n_grid),
+        functools.partial(gather_kernel, nx, nz, n_grid),
         out_shape=(
-            jax.ShapeDtypeStruct((nq, np_ * BANDS), f32),
-            jax.ShapeDtypeStruct((ROUNDS, rp, BLOCK), f32),
+            jax.ShapeDtypeStruct((nq, n), f32),
+            jax.ShapeDtypeStruct((n, n), f32),
+            jax.ShapeDtypeStruct((np_, k), f32),
         ),
         in_specs=[pl.BlockSpec(memory_space=pltpu.VMEM)] * 2,
-        out_specs=(pl.BlockSpec(memory_space=pltpu.VMEM),) * 2,
+        out_specs=(pl.BlockSpec(memory_space=pltpu.VMEM),) * 3,
         scratch_shapes=[
             pltpu.VMEM((BANDS - 1, np_, k), f32),
             pltpu.VMEM((nq + np_, 3 * k), jnp.bfloat16),
@@ -306,120 +431,30 @@
             pltpu.VMEM((ROUNDS, nx - 1, nz, rq + rp, BLOCK), f32),
             pltpu.VMEM((ROUNDS, nz - 1, rq + rp, BLOCK), f32),
             pltpu.VMEM((ROUNDS, CORES, pieces, rq, BLOCK), f32),
-            pltpu.SemaphoreType.DMA((6,)),
-            pltpu.SemaphoreType.DMA((6,)),
-            pltpu.SemaphoreType.DMA((6, ROUNDS)),
-            pltpu.SemaphoreType.DMA((6, ROUNDS)),
+            pltpu.VMEM((ROUNDS, rp, BLOCK), f32),
+            pltpu.VMEM((ROUNDS, CORES, BLOCK, k), f32),
+            pltpu.VMEM((BANDS - 1, CORES, BLOCK, k), f32),
+            pltpu.VMEM((3 * nq, n), jnp.bfloat16),
+            pltpu.VMEM((BANDS, BANDS, KEPT, rp, BLOCK), f32),
+            pltpu.VMEM((CORES, nx, nz, BANDS, KEPT, rp, BLOCK), f32),
+            dma((6,)),
+            dma((6,)),
+            dma((6, ROUNDS)),
+            dma((6, ROUNDS)),
+            dma((5,)),
+            dma((5,)),
+            dma((5,)),
+            dma((nz - 1,)),
+            dma((2, nz)),
+            dma((3,)),
         ],
         compiler_params=pltpu.CompilerParams(
-            collective_id=0, has_side_effects=True, vmem_limit_bytes=56 * 1024 * 1024
+            collective_id=0, has_side_effects=True, vmem_limit_bytes=58 * 1024 * 1024
         ),
         cost_estimate=pl.CostEstimate(
             flops=60 * 1024**3, bytes_accessed=8 * 1024 * 1024, transcendentals=0
         ),
     )(basis, panel)
-
-
-def gram_kernel(
-    nx, nz,
-    coeffs_ref, own_ref,
-    gram_ref,
-    rhs, square, to_y, from_y, gathered,
-    send, recv,
-):
-    me = Place(nx, nz)
-    me.barrier()
-    nq, n = coeffs_ref.shape
-    rp = own_ref.shape[1]
-    np_ = n // BANDS
-    count = BANDS * rp
-
-    high, low = halves(coeffs_ref[...])
-    rhs[:nq, :] = high
-    rhs[nq : 2 * nq, :] = low
-    rhs[2 * nq :, :] = high
-    row = lax.broadcasted_iota(jnp.int32, (count, n), 0)
-    col = lax.broadcasted_iota(jnp.int32, (count, n), 1)
-    want = lax.div(row, rp) * np_ + lax.rem(row, rp) + me.at * rp
-    pick = jnp.where(col == want, 1.0, 0.0).astype(jnp.bfloat16)
-    high = dot_nt(pick, rhs[:nq, :]).astype(jnp.bfloat16)
-    low = dot_nt(pick, rhs[nq : 2 * nq, :]).astype(jnp.bfloat16)
-    square[...] = jnp.dot(
-        jnp.concatenate([high, high, low], 1), rhs[...], preferred_element_type=jnp.float32
-    )
-    for band in range(BANDS):
-        for q in range(ROUNDS):
-            at = pl.multiple_of(tile_of(band, me.core, q) * BLOCK, BLOCK)
-            to_y[band, q] = square[band * rp : (band + 1) * rp, pl.ds(at, BLOCK)]
-    for d, band, device in me.over_y():
-        remote(to_y.at[band], from_y.at[d], send.at[0], recv.at[0], device).start()
-    total = own_ref[...] - to_y[me.band]
-    await_bytes(from_y, recv.at[0])
-    for d in range(BANDS - 1):
-        total = total - from_y[d]
-    here = gathered.at[me.core, me.x, me.z, me.band]
-    gathered[me.core, me.x, me.z, me.band] = total
-    for _, _, device in me.over_y():
-        remote(here, here, send.at[1], recv.at[1], device).start()
-    await_bytes(from_y, recv.at[1])
-    here = gathered.at[me.core, me.x, me.z]
-    for _, _, device in me.over_z():
-        remote(here, here, send.at[2], recv.at[2], device).start()
-    await_bytes(gathered.at[0, 0, pl.ds(0, nz - 1)], recv.at[2])
-    here = gathered.at[me.core, me.x]
-    for _, _, device in me.over_x():
-        remote(here, here, send.at[3], recv.at[3], device).start()
-    await_bytes(gathered.at[0, pl.ds(0, nx - 1)], recv.at[3])
-    here = gathered.at[me.core]
-    remote(here, here, send.at[4], recv.at[4], me.other_core()).start()
-    await_bytes(gathered.at[0], recv.at[4])
-    for band in range(BANDS):
-        for core in range(CORES):
-            for q in range(ROUNDS):
-                at = int(static_tile(band, core, q)) * BLOCK
-                gram_ref[band * np_ : (band + 1) * np_, at : at + BLOCK] = gathered[
-                    core, :, :, band, q
-                ].reshape(np_, BLOCK)
-    await_bytes(from_y, send.at[0])
-    await_bytes(from_y, send.at[1])
-    await_bytes(gathered.at[0, 0, pl.ds(0, nz - 1)], send.at[2])
-    await_bytes(gathered.at[0, pl.ds(0, nx - 1)], send.at[3])
-    await_bytes(gathered.at[0], send.at[4])
-
-
-def static_tile(band, core, turn):
-    if turn == 0:
-        return 2 * band + core
-    if turn == 3:
-        return 2 * ((band + 2) % BANDS) + core
-    return 2 * ((band + (3 if core else 1)) % BANDS) + turn - 1
-
-
-def gather_gram(nx, nz, coeffs, own):
-    nq, n = coeffs.shape
-    rp = own.shape[1]
-    f32 = jnp.float32
-    return pl.pallas_call(
-        functools.partial(gram_kernel, nx, nz),
-        out_shape=jax.ShapeDtypeStruct((n, n), f32),
-        in_specs=[pl.BlockSpec(memory_space=pltpu.VMEM)] * 2,
-        out_specs=pl.BlockSpec(memory_space=pltpu.VMEM),
-        scratch_shapes=[
-            pltpu.VMEM((3 * nq, n), jnp.bfloat16),
-            pltpu.VMEM((BANDS * rp, n), f32),
-            pltpu.VMEM((BANDS, ROUNDS, rp, BLOCK), f32),
-            pltpu.VMEM((BANDS - 1, ROUNDS, rp, BLOCK), f32),
-            pltpu.VMEM((CORES, nx, nz, BANDS, ROUNDS, rp, BLOCK), f32),
-            pltpu.SemaphoreType.DMA((5,)),
-            pltpu.SemaphoreType.DMA((5,)),
-        ],
-        compiler_params=pltpu.CompilerParams(
-            collective_id=1, has_side_effects=True, vmem_limit_bytes=40 * 1024 * 1024
-        ),
-        cost_estimate=pl.CostEstimate(
-            flops=40 * 1024**3, bytes_accessed=8 * 1024 * 1024, transcendentals=0
-        ),
-    )(coeffs, own)
 
 
 def block_inverse(tiles):
@@ -548,26 +583,7 @@
     n_grid = panel.shape[1] * grid
     rows_p = panel.shape[0]
     nz = grid // (CORES * ALONG_X)
-    coeffs, own = reduce_products(ALONG_X, nz, n_grid, basis, panel)
-    gram = gather_gram(ALONG_X, nz, coeffs, own)
-
-    bits = [1 << i for i in range(band.bit_length() - 1)]
-    odd = at_band % 2
-
-    def removed_rows(which):
-        cols = [
-            lax.dynamic_slice_in_dim(coeffs, (which + i) * rows_p, rows_p, 1)
-            for i in range(0, band, 2)
-        ]
-        return cdot(jnp.concatenate(cols, 1), basis).reshape(band // 2, rows_p, -1)
-
-    kept = removed_rows(odd) + swap(removed_rows(1 - odd), band, 1)
-    for bit in bits[1:]:
-        halves_of = kept.reshape(-1, 2, rows_p, kept.shape[-1])
-        side = (at_band // bit) % 2
-        sent = lax.dynamic_index_in_dim(halves_of, 1 - side, 1, keepdims=False)
-        kept = lax.dynamic_index_in_dim(halves_of, side, 1, keepdims=False) + swap(sent, band, bit)
-    projected = panel - kept.reshape(panel.shape)
+    coeffs, gram, projected = reduce_and_project(ALONG_X, nz, n_grid, basis, panel)
     projected, gram = lax.optimization_barrier((projected, gram))
     others = [projected] + [swap(projected, band, d) for d in range(1, band)]
     inverse = inverse_factor(gram)

time: 277 us -> 193 us (0.70)
  waiting for transfers between devices: 45.6 us -> 0.01 us
  Pallas kernels: 206 us -> 176 us
  other arithmetic: 3.96 us -> 0 us
    ppermute x5 -> x3, waiting for transfers between devices: 45.6 us -> 0.01 us  [swap(): return lax.ppermute(x, 'band', [(i, i ^ bit) for i in range(band)])]
    pallas_call x2 -> x1, Pallas kernels: 150 us -> 120 us  [reduce_and_project(): pl.pallas_call(functools.partial(gather_kernel, nx, nz, n_grid), out_shap...]
    dot_general x2 -> x0, matrix products: 5.13 us -> none  [cdot(): lax.dot_general(left, right, (((0,), (0,)), ((), ())), precision=lax.Prec...]
    dot_general x4, matrix products: 3.59 us -> 8.08 us  [body(): new_panel = new_panel + jnp.dot(cols, rows, precision=lax.Precision.HIGH)]
  transfers between devices with their start and end apart: 5 -> 3, of which waited for: 1 -> 0; matrix products, arithmetic and copies ran while one was open for 1% -> 3% of each run, Pallas kernels for 46% -> 29%
where the time goes in v2:
time: 193 us
  Pallas kernels  176 us (91%)
  matrix products  8.08 us (4%)
  local copies, waits for them, and re-layouts  5.45 us (3%)
  starting transfers between devices  3.34 us (2%)
    pallas_call x1, Pallas kernels, reduce_and_project(): pl.pallas_call(functools.partial(gather_kernel, nx, nz, n_grid), out_shap...  120 us
    pallas_call x1, Pallas kernels, inverse_factor(): pl.pallas_call(factor_kernel, out_shape=jax.ShapeDtypeStruct((n, n), jnp....  55.6 us
    dot_general x4, matrix products, body(): new_panel = new_panel + jnp.dot(cols, rows, precision=lax.Precision.HIGH)  8.08 us
    unnamed x9, local copies, waits for them, and re-layouts  5.45 us
  transfers between devices with their start and end apart: 3, of which 0 were waited for; matrix products, arithmetic and copies ran while one was open for 3% of the time, Pallas kernels for 29%

profile of v2, /device:TPU:1, one launch (start us, length us, event | category | flops | bytes accessed | tf_op | source)
XLA Modules:
  0.0 193.2 jit_solution(2309646004016837064)
XLA Ops:
  0.6 119.9 %shard_map.41 = (f32[512,1024]{1,0:T(8,128)}, f32[1024,1024]{1,0:T(8,128)}, f32[256,1024]{1,0:T(8,128)}) custom-call(f32[512,1024]{1,0:T(8,128)} %basis_ref.1, f32[256,1024]{1,0:T(8,128)} %panel_ref.1), custom_call_target="tpu_custom_call" | custom-call | flops 64424509440 | bytes 8388608 | tf_op jit(solution)/shard_map/pallas_call | solution.py:416
  120.6 0.4 collective-permute-start
  121.0 2.2 %collective-permute-start.2 = (f32[256,1024]{1,0:T(8,128)}, f32[256,1024]{1,0:T(8,128)}, u32[]{:S(2)}, u32[]{:S(2)}) collective-permute-start(f32[256,1024]{1,0:T(8,128)} %get-tuple-element.10), channel_id=1, source_target_pairs={{0,3},{1,2},{2,1},{3,0},{4,7},{5,6},{6,5},{7,4},{8,11},{9,10},{10,... | collective-permute-start | bytes 3145736 | tf_op jit(solution)/shard_map/ppermute | solution.py:577
  123.2 0.7 collective-permute-start.1
  123.9 0.0 copy-start.1
  123.9 2.2 %copy-done.1 = f32[1024,1024]{1,0:T(8,128)S(1)} copy-done((f32[1024,1024]{1,0:T(8,128)S(1)}, f32[1024,1024]{1,0:T(8,128)}, u32[]{:S(2)}) %copy-start.1) | copy-done | bytes 4194328
  126.1 0.0 copy-start.3
  126.1 55.6 %shard_map.42 = f32[1024,1024]{1,0:T(8,128)S(1)} custom-call(f32[1024,1024]{1,0:T(8,128)S(1)} %copy-done.1), custom_call_target="tpu_custom_call" | custom-call | flops 64424509440 | bytes 8388608 | tf_op jit(solution)/shard_map/pallas_call | solution.py:560
  181.8 0.0 copy-start
  181.8 1.9 copy-done
  183.7 0.0 copy-done.3
  183.7 1.6 fusion.5
  185.4 0.0 collective-permute-done.2
  185.4 2.0 %fusion.1 = f32[256,1024]{1,0:T(8,128)S(1)} fusion(f32[256,1024]{1,0:T(8,128)} %collective-permute-done.2, f32[1024,1024]{1,0:T(8,128)} %copy-done, s32[]{:T(128)S(6)} %select_n.22, s32[]{:T(128)S(6)} %select_n.28), kind=kOutput, calls=%fused_computation.3 | convolution fusion | flops 402653184 | bytes 2359304 | tf_op jit(solution)/shard_map/dot_general | solution.py:594
  187.4 0.0 copy-start.2
  187.4 0.0 collective-permute-done
  187.4 1.8 convolution_add_fusion.1
  189.2 0.0 collective-permute-done.1
  189.2 2.7 %fusion = f32[256,1024]{1,0:T(8,128)} fusion(f32[256,1024]{1,0:T(8,128)S(1)} %fusion.1, f32[256,1024]{1,0:T(8,128)S(1)} %convolution_add_fusion.1, f32[256,1024]{1,0:T(8,128)S(1)} %collective-permute-done.1, f32[1024,1024]{1,0:T(8,128)} %copy-done, s32[]{:T(128)S(6)} %select_n.22, s32[]{:T(128)S(6)} %select_n.26), kind=kOutput, calls=%fused_computation.1 | convolution fusion | flops 403177472 | bytes 4456456 | tf_op jit(solution)/shard_map/dot_general | solution.py:594
  191.9 0.0 copy-done.2
  191.9 1.3 copy.5
Async XLA Ops:
  120.6 66.8 %collective-permute-start = (f32[256,1024]{1,0:T(8,128)}, f32[256,1024]{1,0:T(8,128)S(1)}, u32[]{:S(2)}, u32[]{:S(2)}) collective-permute-start(f32[256,1024]{1,0:T(8,128)} %get-tuple-element.10), channel_id=1, source_target_pairs={{0,1},{1,0},{2,3},{3,2},{4,5},{5,4},{6,7},{7,6},{8,9},{9,8},{10,11... | collective-permute-start | bytes 3145736 | tf_op jit(solution)/shard_map/ppermute | solution.py:577
  121.0 64.4 %collective-permute-start.2 = (f32[256,1024]{1,0:T(8,128)}, f32[256,1024]{1,0:T(8,128)}, u32[]{:S(2)}, u32[]{:S(2)}) collective-permute-start(f32[256,1024]{1,0:T(8,128)} %get-tuple-element.10), channel_id=1, source_target_pairs={{0,3},{1,2},{2,1},{3,0},{4,7},{5,6},{6,5},{7,4},{8,11},{9,10},{10,... | collective-permute-start | bytes 3145736 | tf_op jit(solution)/shard_map/ppermute | solution.py:577
  123.2 66.0 %collective-permute-start.1 = (f32[256,1024]{1,0:T(8,128)}, f32[256,1024]{1,0:T(8,128)S(1)}, u32[]{:S(2)}, u32[]{:S(2)}) collective-permute-start(f32[256,1024]{1,0:T(8,128)} %get-tuple-element.10), channel_id=1, source_target_pairs={{0,2},{1,3},{2,0},{3,1},{4,6},{5,7},{6,4},{7,5},{8,10},{9,11},{10,... | collective-permute-start | bytes 3145736 | tf_op jit(solution)/shard_map/ppermute | solution.py:577
  123.9 2.2 %copy-start.1 = (f32[1024,1024]{1,0:T(8,128)S(1)}, f32[1024,1024]{1,0:T(8,128)}, u32[]{:S(2)}) copy-start(f32[1024,1024]{1,0:T(8,128)} %get-tuple-element.9.gram_ref) | copy-start | bytes 12582916
  126.1 57.6 %copy-start.3 = (f32[256,1024]{1,0:T(8,128)S(1)}, f32[256,1024]{1,0:T(8,128)}, u32[]{:S(2)}) copy-start(f32[256,1024]{1,0:T(8,128)} %get-tuple-element.10) | copy-start | bytes 3145732
  181.8 1.9 %copy-start = (f32[1024,1024]{1,0:T(8,128)}, f32[1024,1024]{1,0:T(8,128)S(1)}, u32[]{:S(2)}) copy-start(f32[1024,1024]{1,0:T(8,128)S(1)} %shard_map.42) | copy-start | bytes 12582916
  187.4 4.5 %copy-start.2 = (f32[512,1024]{1,0:T(8,128)S(1)}, f32[512,1024]{1,0:T(8,128)}, u32[]{:S(2)}) copy-start(f32[512,1024]{1,0:T(8,128)} %get-tuple-element.15) | copy-start | bytes 6291460

commit v3 on v2

--- a/solution.py
+++ b/solution.py
@@ -13,6 +13,8 @@
 BANDS = 4
 ROUNDS = 4
 KEPT = 3
+GROUP = 4
+MIDWAY = 5
 ALONG_X = 4
 MESH = pl.DeviceIdType.MESH
 
@@ -107,13 +109,151 @@
     pltpu.make_async_copy(ref, ref, sem).wait()
 
 
+def across_lanes(tile, lane):
+    return jnp.broadcast_to(tile[:, lane : lane + 1], (ROWS, BLOCK))
+
+
+def down_rows(tile, row):
+    return jnp.broadcast_to(tile[row : row + 1, :], (ROWS, BLOCK))
+
+
+def block_inverse(tiles):
+    lanes = lax.broadcasted_iota(jnp.int32, (ROWS, BLOCK), 1)
+    subs = lax.broadcasted_iota(jnp.int32, (ROWS, BLOCK), 0)
+    tiles = list(tiles)
+    count = len(tiles)
+    done = []
+    outs = []
+    square = [across_lanes(tiles[0], q) for q in range(ROWS)]
+    for t in range(count):
+        base = ROWS * t
+        here = (lanes >= base) & (lanes < base + ROWS)
+        more = t + 1 < count
+        if more:
+            ahead = tiles[t + 1]
+            side = [across_lanes(ahead, base + q) for q in range(ROWS)]
+            following = [across_lanes(ahead, base + ROWS + q) for q in range(ROWS)]
+        far = t + 2 < min(count, (t // GROUP + 1) * GROUP + 1)
+        if far:
+            beyond = tiles[t + 2]
+            wing = [across_lanes(beyond, base + q) for q in range(ROWS)]
+        current = jnp.where(here, jnp.where(lanes - base == subs, 1.0, 0.0), tiles[t])
+        rows, scaled, unit = [], [], {}
+        out = None
+        for q in range(ROWS):
+            root = lax.rsqrt(down_rows(square[q], q))
+            inv = root * root
+            scaled.append(inv)
+            row = down_rows(current, q)
+            rows.append(row)
+            out = row * root if q == 0 else jnp.where(subs == q, row * root, out)
+            if q + 1 < ROWS:
+                current = current - (square[q] * inv) * row
+            for s in range(q + 1, ROWS):
+                unit[s, q] = down_rows(square[q], s) * inv
+                square[s] = square[s] - unit[s, q] * square[q]
+            if far:
+                for s in range(q + 1, ROWS):
+                    wing[s] = wing[s] - unit[s, q] * wing[q]
+                beyond = (jnp.where(here, 0.0, beyond) if q == 0 else beyond) - (wing[q] * inv) * row
+            if more:
+                weight = side[q] * inv
+                for s in range(q + 1, ROWS):
+                    side[s] = side[s] - unit[s, q] * side[q]
+                for s in range(ROWS):
+                    following[s] = following[s] - weight * down_rows(side[q], s)
+                ahead = (jnp.where(here, 0.0, ahead) if q == 0 else ahead) - weight * row
+        if far:
+            tiles[t + 2] = beyond
+        done.append(jnp.where(lanes <= base + subs, out, 0.0))
+        ends = (t // GROUP + 1) * GROUP * ROWS
+        outs.append((out, jnp.where((lanes < base + ROWS) | (lanes >= ends), out, 0.0)))
+        if more:
+            square = following
+            tiles[t + 1] = ahead
+        if t + 3 < min(count, (t // GROUP + 1) * GROUP + 1):
+            back = [rows[p] * scaled[p] for p in range(ROWS)]
+            for p in range(ROWS - 1, 0, -1):
+                for q in range(p):
+                    back[q] = back[q] - unit[p, q] * back[p]
+            for u in range(t + 3, min(count, (t // GROUP + 1) * GROUP + 1)):
+                old = tiles[u]
+                new = jnp.where(here, 0.0, old)
+                for p in range(ROWS):
+                    new = new - across_lanes(old, base + p) * back[p]
+                tiles[u] = new
+        first = t + 1 + 1
+        if (t + 1) % GROUP == 0 and first < count:
+            high, low = halves(jnp.concatenate([o[0] for o in outs[t + 1 - GROUP :]], 0))
+            rhigh, rlow = halves(jnp.concatenate([o[1] for o in outs[t + 1 - GROUP :]], 0))
+            change = lax.dot_general(
+                jnp.concatenate([high, high, low], 0),
+                jnp.concatenate([rhigh, rlow, rhigh], 0),
+                (((0,), (0,)), ((), ())),
+                preferred_element_type=jnp.float32,
+            )
+            group = (lanes >= base + ROWS - GROUP * ROWS) & (lanes < base + ROWS)
+            for u in range(first, count):
+                tiles[u] = jnp.where(group, 0.0, tiles[u]) - change[u * ROWS : (u + 1) * ROWS]
+    return done
+
+
+def factor_steps(a_ref, diag_ref, diag_right, lower_ref, right_ref, midway):
+    n = a_ref.shape[0]
+    blocks = n // BLOCK
+    wide = 2 * BLOCK
+    diag_right[...] = jnp.zeros_like(diag_right)
+    right_ref[...] = jnp.zeros_like(right_ref)
+
+    def step(k, carry):
+        pl.when(k == MIDWAY)(midway)
+        at = pl.ds(pl.multiple_of(k * BLOCK, BLOCK), BLOCK)
+        before = pl.ds(pl.multiple_of(jnp.maximum(k - 1, 0) * BLOCK, BLOCK), BLOCK)
+        after = pl.ds(pl.multiple_of(jnp.minimum(k + 1, blocks - 1) * BLOCK, BLOCK), BLOCK)
+        base = pl.multiple_of(k * BLOCK, BLOCK)
+        tiles = [a_ref[pl.ds(base + ROWS * t, ROWS), at] for t in range(BLOCK // ROWS)]
+
+        for j in range(2, blocks):
+            rows = slice(j * BLOCK, (j + 1) * BLOCK)
+            on = jnp.where((j > k) & (k > 0), 1.0, 0.0).astype(jnp.float32)
+            old = a_ref[rows, before]
+            lower_ref[rows, :] = left_parts(dot_nt(left_parts(old), diag_right[...]) * on)
+            a_ref[rows, before] = old * (1.0 - on)
+        for c in range(n // wide):
+            cols = slice(c * wide, (c + 1) * wide)
+            for j in range(1, blocks // 2):
+                rows = slice(j * wide, (j + 1) * wide)
+                a_ref[rows, cols] -= jnp.dot(
+                    lower_ref[rows, :], right_ref[:, cols], preferred_element_type=jnp.float32
+                )
+        for t, tile in enumerate(block_inverse(tiles)):
+            diag_ref[ROWS * t : ROWS * (t + 1), :] = tile
+
+        diag = diag_ref[...]
+        a_ref[at, :] = jnp.dot(
+            left_parts(diag), right_parts(a_ref[at, :], 0), preferred_element_type=jnp.float32
+        )
+        a_ref[at, at] = diag
+        right_ref[...] = right_parts(a_ref[at, :], 0)
+        diag_right[...] = right_parts(diag, 1)
+        on = jnp.where(k < blocks - 1, 1.0, 0.0).astype(jnp.float32)
+        old = a_ref[after, at]
+        low = dot_nt(left_parts(old), diag_right[...]) * on
+        a_ref[after, at] = old * (1.0 - on)
+        a_ref[after, :] -= jnp.dot(left_parts(low), right_ref[...], preferred_element_type=jnp.float32)
+        return carry
+
+    lax.fori_loop(0, blocks, step, 0)
+
+
 def gather_kernel(
     nx, nz, n_grid,
     basis_ref, panel_ref,
-    coeffs_ref, gram_ref, projected_ref,
+    coeffs_ref, panel_out_ref,
     others, lhs, rhs, part, from_core, from_x, from_z, gathered, own,
     removed, from_band, stacked, share, pieces_of,
-    y_send, y_recv, send, recv, b_send, b_recv, g_send, z_recv, x_recv, g_recv,
+    gram_ref, diag, diag_right, lower, right_parts_of, projected, projected_others,
+    y_send, y_recv, send, recv, b_send, b_recv, g_send, z_recv, x_recv, g_recv, p_send, p_recv,
 ):
     me = Place(nx, nz)
     me.barrier()
@@ -387,7 +527,51 @@
         total = removed[0, t]
         for d in range(BANDS - 1):
             total = total + from_band[d, t]
-        projected_ref[rows, :] = panel_ref[rows, :] - total
+        projected[rows, :] = panel_ref[rows, :] - total
+
+    def carry(i, src, dst, device):
+        return remote(src, dst, p_send.at[i], p_recv.at[i], device)
+
+    carried = [
+        carry(0, projected.at[lo], projected_others.at[2, lo], right),
+        carry(1, projected.at[lo], projected_others.at[0, lo], left),
+        carry(2, projected.at[hi], projected_others.at[2, hi], right),
+        carry(3, projected.at[hi], projected_others.at[0, hi], left),
+        carry(4, projected_others.at[2, lo], projected_others.at[1, lo], right),
+        carry(5, projected_others.at[0, hi], projected_others.at[1, hi], left),
+    ]
+    for h in carried[:4]:
+        h.start()
+
+    def midway():
+        carried[0].wait_recv()
+        carried[4].start()
+        carried[3].wait_recv()
+        carried[5].start()
+
+    factor_steps(gram_ref, diag, diag_right, lower, right_parts_of, midway)
+    mine = pl.ds(pl.multiple_of(me.band * np_, np_), np_)
+    row = lax.broadcasted_iota(jnp.int32, (np_, np_), 0) + me.band * np_
+    col = lax.broadcasted_iota(jnp.int32, (np_, np_), 1)
+
+    def times(r, block):
+        first = lax.rem(me.band + r, BANDS) * np_
+        tile = gram_ref[mine, pl.ds(pl.multiple_of(first, np_), np_)]
+        tile = jnp.where(col + first <= row, tile, 0.0)
+        return jnp.dot(
+            left_parts(tile), right_parts(block, 0), preferred_element_type=jnp.float32
+        )
+
+    panel_out_ref[...] = times(0, projected[...])
+    carried[1].wait_recv()
+    carried[2].wait_recv()
+    panel_out_ref[...] += times(1, projected_others[0])
+    panel_out_ref[...] += times(3, projected_others[2])
+    carried[4].wait_recv()
+    carried[5].wait_recv()
+    panel_out_ref[...] += times(2, projected_others[1])
+    for h in carried:
+        h.wait_send()
 
     for h in bulks:
         h.wait_send()
@@ -417,11 +601,10 @@
         functools.partial(gather_kernel, nx, nz, n_grid),
         out_shape=(
             jax.ShapeDtypeStruct((nq, n), f32),
-            jax.ShapeDtypeStruct((n, n), f32),
             jax.ShapeDtypeStruct((np_, k), f32),
         ),
         in_specs=[pl.BlockSpec(memory_space=pltpu.VMEM)] * 2,
-        out_specs=(pl.BlockSpec(memory_space=pltpu.VMEM),) * 3,
+        out_specs=(pl.BlockSpec(memory_space=pltpu.VMEM),) * 2,
         scratch_shapes=[
             pltpu.VMEM((BANDS - 1, np_, k), f32),
             pltpu.VMEM((nq + np_, 3 * k), jnp.bfloat16),
@@ -437,6 +620,13 @@
             pltpu.VMEM((3 * nq, n), jnp.bfloat16),
             pltpu.VMEM((BANDS, BANDS, KEPT, rp, BLOCK), f32),
             pltpu.VMEM((CORES, nx, nz, BANDS, KEPT, rp, BLOCK), f32),
+            pltpu.VMEM((n, n), f32),
+            pltpu.VMEM((BLOCK, BLOCK), f32),
+            pltpu.VMEM((BLOCK, 3 * BLOCK), jnp.bfloat16),
+            pltpu.VMEM((n, 3 * BLOCK), jnp.bfloat16),
+            pltpu.VMEM((3 * BLOCK, n), jnp.bfloat16),
+            pltpu.VMEM((np_, k), f32),
+            pltpu.VMEM((BANDS - 1, np_, k), f32),
             dma((6,)),
             dma((6,)),
             dma((6, ROUNDS)),
@@ -447,9 +637,11 @@
             dma((nz - 1,)),
             dma((2, nz)),
             dma((3,)),
+            dma((6,)),
+            dma((6,)),
         ],
         compiler_params=pltpu.CompilerParams(
-            collective_id=0, has_side_effects=True, vmem_limit_bytes=58 * 1024 * 1024
+            collective_id=0, has_side_effects=True, vmem_limit_bytes=60 * 1024 * 1024
         ),
         cost_estimate=pl.CostEstimate(
             flops=60 * 1024**3, bytes_accessed=8 * 1024 * 1024, transcendentals=0
@@ -457,141 +649,12 @@
     )(basis, panel)
 
 
-def block_inverse(tiles):
-    lanes = lax.broadcasted_iota(jnp.int32, (ROWS, BLOCK), 1)
-    subs = lax.broadcasted_iota(jnp.int32, (ROWS, BLOCK), 0)
-    shape = (ROWS, BLOCK)
-    tiles = list(tiles)
-    count = len(tiles)
-    done = []
-    for t in range(count):
-        tile = tiles[t]
-        base = ROWS * t
-        here = (lanes >= base) & (lanes < base + ROWS)
-        cols = [jnp.broadcast_to(tile[:, base + q : base + q + 1], shape) for q in range(ROWS)]
-        entry = {
-            (p, q): jnp.broadcast_to(cols[q][p : p + 1, :], shape)
-            for q in range(ROWS)
-            for p in range(q, ROWS)
-        }
-        start = jnp.where(here, jnp.where(lanes - base == subs, 1.0, 0.0), tile)
-        rows = [jnp.broadcast_to(start[p : p + 1, :], shape) for p in range(ROWS)]
-        unit = {}
-        root = []
-        scaled = []
-        for q in range(ROWS):
-            inv_root = lax.rsqrt(entry[q, q])
-            inv = inv_root * inv_root
-            root.append(inv_root)
-            scaled.append(inv)
-            for p in range(q + 1, ROWS):
-                unit[p, q] = entry[p, q] * inv
-            for p in range(q + 1, ROWS):
-                for s in range(q + 1, p + 1):
-                    entry[p, s] = entry[p, s] - unit[p, q] * entry[s, q]
-                rows[p] = rows[p] - unit[p, q] * rows[q]
-        out = rows[0] * root[0]
-        for p in range(1, ROWS):
-            out = jnp.where(subs == p, rows[p] * root[p], out)
-        done.append(jnp.where(lanes <= base + subs, out, 0.0))
-        if t + 1 < count:
-            back = [rows[p] * scaled[p] for p in range(ROWS)]
-            for p in range(ROWS - 1, 0, -1):
-                for q in range(p):
-                    back[q] = back[q] - unit[p, q] * back[p]
-            for u in range(t + 1, count):
-                old = tiles[u]
-                new = jnp.where(here, 0.0, old)
-                for p in range(ROWS):
-                    new = new - jnp.broadcast_to(old[:, base + p : base + p + 1], shape) * back[p]
-                tiles[u] = new
-    return done
-
-
-def factor_kernel(gram_ref, out_ref, diag_ref, right_ref):
-    blocks = out_ref.shape[0] // BLOCK
-    out_ref[...] = gram_ref[...]
-
-    def step(k, carry):
-        at = pl.ds(pl.multiple_of(k * BLOCK, BLOCK), BLOCK)
-        base = pl.multiple_of(k * BLOCK, BLOCK)
-        tiles = [
-            out_ref[pl.ds(base + ROWS * t, ROWS), at] for t in range(BLOCK // ROWS)
-        ]
-        for t, tile in enumerate(block_inverse(tiles)):
-            diag_ref[pl.ds(ROWS * t, ROWS), :] = tile
-        diag = diag_ref[...]
-        panel = jnp.dot(
-            left_parts(diag),
-            right_parts(out_ref[at, :], 0),
-            preferred_element_type=jnp.float32,
-        )
-        out_ref[at, :] = panel
-        out_ref[at, at] = diag
-        right_ref[...] = right_parts(out_ref[at, :], 0)
-        diag_right = right_parts(diag, 1)
-
-        def update(i, carry):
-            rows = pl.ds(pl.multiple_of(i * BLOCK, BLOCK), BLOCK)
-            lower = dot_nt(left_parts(out_ref[rows, at]), diag_right)
-            out_ref[rows, at] = jnp.zeros((BLOCK, BLOCK), jnp.float32)
-            out_ref[rows, :] -= jnp.dot(
-                left_parts(lower), right_ref[...], preferred_element_type=jnp.float32
-            )
-            return carry
-
-        lax.fori_loop(k + 1, blocks, update, 0)
-        return carry
-
-    lax.fori_loop(0, blocks, step, 0)
-    row = lax.broadcasted_iota(jnp.int32, (BLOCK, out_ref.shape[1]), 0)
-    col = lax.broadcasted_iota(jnp.int32, (BLOCK, out_ref.shape[1]), 1)
-
-    def clear(i, carry):
-        rows = pl.ds(pl.multiple_of(i * BLOCK, BLOCK), BLOCK)
-        out_ref[rows, :] = jnp.where(col <= row + i * BLOCK, out_ref[rows, :], 0.0)
-        return carry
-
-    lax.fori_loop(0, blocks, clear, 0)
-
-
-def inverse_factor(gram):
-    n = gram.shape[0]
-    return pl.pallas_call(
-        factor_kernel,
-        out_shape=jax.ShapeDtypeStruct((n, n), jnp.float32),
-        in_specs=[pl.BlockSpec(memory_space=pltpu.VMEM)],
-        out_specs=pl.BlockSpec(memory_space=pltpu.VMEM),
-        scratch_shapes=[
-            pltpu.VMEM((BLOCK, BLOCK), jnp.float32),
-            pltpu.VMEM((3 * BLOCK, n), jnp.bfloat16),
-        ],
-        compiler_params=pltpu.CompilerParams(vmem_limit_bytes=32 * 1024 * 1024),
-        cost_estimate=pl.CostEstimate(
-            flops=60 * n * n * n, bytes_accessed=8 * n * n, transcendentals=n
-        ),
-    )(gram)
-
-
-def swap(x, band, bit):
-    return lax.ppermute(x, "band", [(i, i ^ bit) for i in range(band)])
-
-
 def body(basis, panel):
-    grid, band = lax.axis_size("grid"), lax.axis_size("band")
-    at_band = lax.axis_index("band")
-    n_grid = panel.shape[1] * grid
-    rows_p = panel.shape[0]
+    grid = lax.axis_size("grid")
     nz = grid // (CORES * ALONG_X)
-    coeffs, gram, projected = reduce_and_project(ALONG_X, nz, n_grid, basis, panel)
-    projected, gram = lax.optimization_barrier((projected, gram))
-    others = [projected] + [swap(projected, band, d) for d in range(1, band)]
-    inverse = inverse_factor(gram)
-    inverse_rows = lax.dynamic_slice_in_dim(inverse, at_band * rows_p, rows_p, 0)
-    new_panel = 0.0
-    for d, rows in enumerate(others):
-        cols = lax.dynamic_slice_in_dim(inverse_rows, (at_band ^ d) * rows_p, rows_p, 1)
-        new_panel = new_panel + jnp.dot(cols, rows, precision=lax.Precision.HIGH)
+    coeffs, new_panel = reduce_and_project(
+        ALONG_X, nz, panel.shape[1] * grid, basis, panel
+    )
     return (new_panel, coeffs)
 
 

time: 193 us -> 161 us (0.83)
  Pallas kernels: 176 us -> 157 us
  matrix products: 8.08 us -> 0 us
  starting transfers between devices: 3.34 us -> 0 us
    pallas_call x1 -> x0, Pallas kernels: 55.6 us -> none  [inverse_factor(): pl.pallas_call(factor_kernel, out_shape=jax.ShapeDtypeStruct((n, n), jnp....]
    pallas_call x1, Pallas kernels: 120 us -> 157 us  [reduce_and_project(): pl.pallas_call(functools.partial(gather_kernel, nx, nz, n_grid), out_shap...]
    dot_general x4 -> x0, matrix products: 8.08 us -> none  [body(): new_panel = new_panel + jnp.dot(cols, rows, precision=lax.Precision.HIGH)]
    ppermute x3 -> x0, starting transfers between devices: 3.34 us -> none  [swap(): return lax.ppermute(x, 'band', [(i, i ^ bit) for i in range(band)])]
    unnamed x9 -> x4, local copies, waits for them, and re-layouts: 5.45 us -> 3.78 us
  transfers between devices with their start and end apart: 3 -> 0, of which waited for: 0 -> 0; matrix products, arithmetic and copies ran while one was open for 3% -> 0% of each run, Pallas kernels for 29% -> 0%
where the time goes in v3:
time: 161 us
  Pallas kernels  157 us (98%)
  local copies, waits for them, and re-layouts  3.78 us (2%)
    pallas_call x1, Pallas kernels, reduce_and_project(): pl.pallas_call(functools.partial(gather_kernel, nx, nz, n_grid), out_shap...  157 us
    unnamed x4, local copies, waits for them, and re-layouts  3.78 us

profile of v3, /device:TPU:1, one launch (start us, length us, event | category | flops | bytes accessed | tf_op | source)
XLA Modules:
  0.0 161.2 jit_solution(424316306353654457)
XLA Ops:
  0.6 156.8 %shard_map.41 = (f32[512,1024]{1,0:T(8,128)}, f32[256,1024]{1,0:T(8,128)}) custom-call(f32[512,1024]{1,0:T(8,128)} %basis_ref.1, f32[256,1024]{1,0:T(8,128)} %panel_ref.1), custom_call_target="tpu_custom_call" | custom-call | flops 64424509440 | bytes 8388608 | tf_op jit(solution)/shard_map/pallas_call | solution.py:600
  157.5 0.0 copy-start
  157.5 2.5 %copy.6 = f32[256,1024]{1,0:T(8,128)} copy(f32[256,1024]{1,0:T(8,128)} %get-tuple-element.8) | data formatting | bytes 2097152
  159.9 0.0 copy-done
  159.9 1.3 copy.7
Async XLA Ops:
  157.5 2.5 %copy-start = (f32[512,1024]{1,0:T(8,128)S(1)}, f32[512,1024]{1,0:T(8,128)}, u32[]{:S(2)}) copy-start(f32[512,1024]{1,0:T(8,128)} %get-tuple-element.9) | copy-start | bytes 6291460

commit v4 on v3

--- a/solution.py
+++ b/solution.py
@@ -14,7 +14,8 @@
 ROUNDS = 4
 KEPT = 3
 GROUP = 4
-MIDWAY = 5
+EARLY = 1
+MIDWAY = 4
 ALONG_X = 4
 MESH = pl.DeviceIdType.MESH
 
@@ -46,9 +47,9 @@
     if turn == 0:
         return 2 * band + core
     if turn == 1:
-        return 2 * (one + core * (three - one))
+        return 2 * (three + core * (one - three)) + core
     if turn == 2:
-        return 2 * (three + core * (one - three)) + 1
+        return 2 * (one + core * (three - one)) + core
     return 2 * two + core
 
 
@@ -198,7 +199,7 @@
     return done
 
 
-def factor_steps(a_ref, diag_ref, diag_right, lower_ref, right_ref, midway):
+def factor_steps(a_ref, diag_ref, diag_right, lower_ref, right_ref, early, midway):
     n = a_ref.shape[0]
     blocks = n // BLOCK
     wide = 2 * BLOCK
@@ -206,6 +207,7 @@
     right_ref[...] = jnp.zeros_like(right_ref)
 
     def step(k, carry):
+        pl.when(k == EARLY)(early)
         pl.when(k == MIDWAY)(midway)
         at = pl.ds(pl.multiple_of(k * BLOCK, BLOCK), BLOCK)
         before = pl.ds(pl.multiple_of(jnp.maximum(k - 1, 0) * BLOCK, BLOCK), BLOCK)
@@ -248,14 +250,19 @@
 
 def gather_kernel(
     nx, nz, n_grid,
-    basis_ref, panel_ref,
-    coeffs_ref, panel_out_ref,
+    basis_in, panel_in,
+    coeffs_out, panel_out,
+    basis_ref, panel_ref, coeffs_ref,
     others, lhs, rhs, part, from_core, from_x, from_z, gathered, own,
     removed, from_band, stacked, share, pieces_of,
     gram_ref, diag, diag_right, lower, right_parts_of, projected, projected_others,
-    y_send, y_recv, send, recv, b_send, b_recv, g_send, z_recv, x_recv, g_recv, p_send, p_recv,
+    y_send, y_recv, send, recv, b_send, b_recv, g_send, z_recv, x_recv, g_recv, p_send, p_recv, io_sem,
 ):
     me = Place(nx, nz)
+    fetch_panel = pltpu.make_async_copy(panel_in, panel_ref, io_sem.at[0])
+    fetch_basis = pltpu.make_async_copy(basis_in, basis_ref, io_sem.at[1])
+    fetch_panel.start()
+    fetch_basis.start()
     me.barrier()
     nq, k = basis_ref.shape
     np_ = panel_ref.shape[0]
@@ -271,14 +278,16 @@
 
     hops = [
         hop(0, panel_ref.at[lo], others.at[2, lo], right),
-        hop(1, panel_ref.at[lo], others.at[0, lo], left),
+        hop(1, panel_ref.at[hi], others.at[0, hi], left),
         hop(2, panel_ref.at[hi], others.at[2, hi], right),
-        hop(3, panel_ref.at[hi], others.at[0, hi], left),
+        hop(3, panel_ref.at[lo], others.at[0, lo], left),
         hop(4, others.at[2, lo], others.at[1, lo], right),
         hop(5, others.at[0, hi], others.at[1, hi], left),
     ]
+    fetch_panel.wait()
     for h in hops[:4]:
         h.start()
+    fetch_basis.wait()
 
     high, low = halves(basis_ref[...])
     lhs[:nq, :k] = high
@@ -375,17 +384,16 @@
         out = out + jnp.dot(high, lhs[:nq, 2 * k :], preferred_element_type=jnp.float32)
         removed[q] = out.reshape(CORES, BLOCK, k)
 
-    across = {"grid": me.grid, "band": lax.rem(me.band + 2, BANDS)}
-
     def bulk(i, src, dst, device):
         return remote(src, dst, b_send.at[i], b_recv.at[i], device)
 
     bulks = [
-        bulk(0, removed.at[1, 0], from_band.at[0, 0], right),
-        bulk(1, removed.at[1, 1], from_band.at[2, 0], left),
-        bulk(2, removed.at[2, 0], from_band.at[2, 1], left),
-        bulk(3, removed.at[2, 1], from_band.at[0, 1], right),
-        bulk(4, removed.at[3], from_band.at[1], across),
+        bulk(0, removed.at[1, 0], from_band.at[2, 0], left),
+        bulk(1, removed.at[1, 1], from_band.at[0, 1], right),
+        bulk(2, removed.at[3, 0], from_band.at[1, 0], right),
+        bulk(3, removed.at[3, 1], from_band.at[1, 1], left),
+        bulk(4, removed.at[2, 0], from_band.at[0, 0], right),
+        bulk(5, removed.at[2, 1], from_band.at[2, 1], left),
     ]
 
     multiply(0, (panel_ref[lo, :], panel_ref[hi, :]))
@@ -395,16 +403,16 @@
     hops[0].wait_recv()
     hops[4].start()
     hops[1].wait_recv()
-    multiply(1, (others[0, lo, :], others[2, lo, :]))
+    hops[5].start()
+    multiply(1, (others[2, lo, :], others[0, hi, :]))
     to_core(1)
     back_z(0)
     to_x(1)
     back_x(0)
     to_z(1)
+    hops[2].wait_recv()
     hops[3].wait_recv()
-    hops[5].start()
-    hops[2].wait_recv()
-    multiply(2, (others[2, hi, :], others[0, hi, :]))
+    multiply(2, (others[0, lo, :], others[2, hi, :]))
     to_core(2)
     back_z(1)
     back_core(0)
@@ -418,23 +426,25 @@
     back_z(2)
     to_x(3)
     back_core(1)
-    back_x(2)
     finish(0)
-    to_z(3)
-    back_core(2)
     finish(1)
     remove(1)
     bulks[0].start()
     bulks[1].start()
-    back_z(3)
+    back_x(2)
+    to_z(3)
+    back_core(2)
     finish(2)
     remove(2)
+    back_z(3)
+    remove(0)
     back_x(3)
-    remove(0)
     back_core(3)
     for h in hops:
         h.wait_send()
     finish(3)
+    leave_coeffs = pltpu.make_async_copy(coeffs_ref, coeffs_out, io_sem.at[2])
+    leave_coeffs.start()
 
     high, low = halves(coeffs_ref[...])
     stacked[:nq, :] = high
@@ -457,14 +467,13 @@
             first = 2 * ((band + i) % BANDS) * BLOCK
             pair = [rows[:, first + t * BLOCK : first + (t + 1) * BLOCK] for t in range(CORES)]
             share[me.band, band, i] = -jnp.where(me.core == 0, pair[0], pair[1])
-    for i, q in enumerate((0, 1 + me.core, ROUNDS - 1)):
+    for i, q in enumerate((0, 2 - me.core, ROUNDS - 1)):
         share[me.band, me.band, i] += own[q]
     for _, _, device in me.over_y():
         remote(share.at[me.band], share.at[me.band], g_send.at[0], g_recv.at[0], device).start()
+    remove(3)
     bulks[2].start()
     bulks[3].start()
-    remove(3)
-    bulks[4].start()
     await_bytes(share.at[pl.ds(0, BANDS - 1)], g_recv.at[0])
     pieces_of[me.core, me.x, me.z] = (share[0] + share[1]) + (share[2] + share[3])
 
@@ -490,16 +499,23 @@
         remote(here, here, g_send.at[4], g_recv.at[2], me.other_core()).start()
 
     here = pieces_of.at[me.core, me.x, me.z]
-    for d, _, device in me.over_z():
-        remote(here, here, g_send.at[1], z_recv.at[d], device).start()
+    nearest = sorted(range(1, nz), key=lambda d: min(d, nz - d))
+    for d in nearest:
+        device = me.id(lax.rem(me.z + d, nz), me.x, me.core)
+        remote(here, here, g_send.at[1], z_recv.at[d - 1], device).start()
     spread(0, me.z)
     order = [me.z]
-    for i, d in enumerate(sorted(range(1, nz), key=lambda d: min(d, nz - d))):
+    for i, d in enumerate(nearest):
         z = lax.rem(me.z + nz - d, nz)
         await_bytes(pieces_of.at[0, 0, 0], z_recv.at[d - 1])
         spread(i + 1, z)
         relay(i, order[i])
         order.append(z)
+        if i == nz // 2:
+            for t in range(CORES):
+                bulks[2 + t].wait_recv()
+                removed[2, t] += from_band[1, t]
+                bulks[4 + t].start()
     cross(me.x)
     relay(nz - 1, order[nz - 1])
     cross(up)
@@ -520,36 +536,34 @@
     await_bytes(pieces_of.at[0], g_recv.at[2])
     place(0)
     place(1)
-    for h in bulks:
-        h.wait_recv()
-    for t in range(CORES):
-        rows = slice(t * BLOCK, (t + 1) * BLOCK)
-        total = removed[0, t]
-        for d in range(BANDS - 1):
-            total = total + from_band[d, t]
-        projected[rows, :] = panel_ref[rows, :] - total
-
     def carry(i, src, dst, device):
         return remote(src, dst, p_send.at[i], p_recv.at[i], device)
 
     carried = [
         carry(0, projected.at[lo], projected_others.at[2, lo], right),
-        carry(1, projected.at[lo], projected_others.at[0, lo], left),
+        carry(1, projected.at[hi], projected_others.at[0, hi], left),
         carry(2, projected.at[hi], projected_others.at[2, hi], right),
-        carry(3, projected.at[hi], projected_others.at[0, hi], left),
+        carry(3, projected.at[lo], projected_others.at[0, lo], left),
         carry(4, projected_others.at[2, lo], projected_others.at[1, lo], right),
         carry(5, projected_others.at[0, hi], projected_others.at[1, hi], left),
     ]
-    for h in carried[:4]:
-        h.start()
+    def early():
+        for i in (0, 1, 4, 5):
+            bulks[i].wait_recv()
+        for t in range(CORES):
+            rows = slice(t * BLOCK, (t + 1) * BLOCK)
+            total = removed[0, t] + (from_band[0, t] + from_band[2, t])
+            projected[rows, :] = panel_ref[rows, :] - total
+        for h in carried[:4]:
+            h.start()
 
     def midway():
         carried[0].wait_recv()
         carried[4].start()
-        carried[3].wait_recv()
+        carried[1].wait_recv()
         carried[5].start()
 
-    factor_steps(gram_ref, diag, diag_right, lower, right_parts_of, midway)
+    factor_steps(gram_ref, diag, diag_right, lower, right_parts_of, early, midway)
     mine = pl.ds(pl.multiple_of(me.band * np_, np_), np_)
     row = lax.broadcasted_iota(jnp.int32, (np_, np_), 0) + me.band * np_
     col = lax.broadcasted_iota(jnp.int32, (np_, np_), 1)
@@ -562,14 +576,17 @@
             left_parts(tile), right_parts(block, 0), preferred_element_type=jnp.float32
         )
 
-    panel_out_ref[...] = times(0, projected[...])
-    carried[1].wait_recv()
+    panel_ref[...] = times(0, projected[...])
     carried[2].wait_recv()
-    panel_out_ref[...] += times(1, projected_others[0])
-    panel_out_ref[...] += times(3, projected_others[2])
+    carried[3].wait_recv()
+    panel_ref[...] += times(1, projected_others[0])
+    panel_ref[...] += times(3, projected_others[2])
     carried[4].wait_recv()
     carried[5].wait_recv()
-    panel_out_ref[...] += times(2, projected_others[1])
+    panel_ref[...] += times(2, projected_others[1])
+    leave_panel = pltpu.make_async_copy(panel_ref, panel_out, io_sem.at[3])
+    leave_panel.start()
+    leave_coeffs.wait()
     for h in carried:
         h.wait_send()
 
@@ -587,6 +604,7 @@
     await_bytes(pieces_of.at[0, pl.ds(0, 2)], g_send.at[2])
     await_bytes(pieces_of.at[0, 0], g_send.at[3])
     await_bytes(pieces_of.at[0], g_send.at[4])
+    leave_panel.wait()
 
 
 def reduce_and_project(nx, nz, n_grid, basis, panel):
@@ -603,9 +621,12 @@
             jax.ShapeDtypeStruct((nq, n), f32),
             jax.ShapeDtypeStruct((np_, k), f32),
         ),
-        in_specs=[pl.BlockSpec(memory_space=pltpu.VMEM)] * 2,
-        out_specs=(pl.BlockSpec(memory_space=pltpu.VMEM),) * 2,
+        in_specs=[pl.BlockSpec(memory_space=pl.ANY)] * 2,
+        out_specs=(pl.BlockSpec(memory_space=pl.ANY),) * 2,
         scratch_shapes=[
+            pltpu.VMEM((nq, k), f32),
+            pltpu.VMEM((np_, k), f32),
+            pltpu.VMEM((nq, n), f32),
             pltpu.VMEM((BANDS - 1, np_, k), f32),
             pltpu.VMEM((nq + np_, 3 * k), jnp.bfloat16),
             pltpu.VMEM((2 * BLOCK, 3 * k), jnp.bfloat16),
@@ -631,14 +652,15 @@
             dma((6,)),
             dma((6, ROUNDS)),
             dma((6, ROUNDS)),
-            dma((5,)),
-            dma((5,)),
+            dma((6,)),
+            dma((6,)),
             dma((5,)),
             dma((nz - 1,)),
             dma((2, nz)),
             dma((3,)),
             dma((6,)),
             dma((6,)),
+            dma((4,)),
         ],
         compiler_params=pltpu.CompilerParams(
             collective_id=0, has_side_effects=True, vmem_limit_bytes=60 * 1024 * 1024

time: 161 us -> 152 us (0.944)
  Pallas kernels: 157 us -> 147 us
    pallas_call x1, Pallas kernels: 157 us -> 147 us  [reduce_and_project(): pl.pallas_call(functools.partial(gather_kernel, nx, nz, n_grid), out_shap...]
where the time goes in v4:
time: 152 us
  Pallas kernels  147 us (97%)
  local copies, waits for them, and re-layouts  3.78 us (2%)
    pallas_call x1, Pallas kernels, reduce_and_project(): pl.pallas_call(functools.partial(gather_kernel, nx, nz, n_grid), out_shap...  147 us
    unnamed x4, local copies, waits for them, and re-layouts  3.78 us

profile of v4, /device:TPU:1, one launch (start us, length us, event | category | flops | bytes accessed | tf_op | source)
XLA Modules:
  0.0 151.8 jit_solution(1323269059485111091)
XLA Ops:
  0.6 147.4 %shard_map.41 = (f32[512,1024]{1,0:T(8,128)}, f32[256,1024]{1,0:T(8,128)}) custom-call(f32[512,1024]{1,0:T(8,128)} %basis_in.1, f32[256,1024]{1,0:T(8,128)} %panel_in.1), custom_call_target="tpu_custom_call" | custom-call | flops 64424509440 | bytes 8388608 | tf_op jit(solution)/shard_map/pallas_call | solution.py:618
  148.0 0.0 copy-start
  148.0 2.5 %copy.6 = f32[256,1024]{1,0:T(8,128)} copy(f32[256,1024]{1,0:T(8,128)} %get-tuple-element.8) | data formatting | bytes 2097152
  150.5 0.0 copy-done
  150.5 1.3 copy.7
Async XLA Ops:
  148.0 2.5 %copy-start = (f32[512,1024]{1,0:T(8,128)S(1)}, f32[512,1024]{1,0:T(8,128)}, u32[]{:S(2)}) copy-start(f32[512,1024]{1,0:T(8,128)} %get-tuple-element.9) | copy-start | bytes 6291460

commit v5 on v4

--- a/solution.py
+++ b/solution.py
@@ -14,7 +14,7 @@
 ROUNDS = 4
 KEPT = 3
 GROUP = 4
-EARLY = 1
+EARLY = 0
 MIDWAY = 4
 ALONG_X = 4
 MESH = pl.DeviceIdType.MESH
@@ -251,8 +251,8 @@
 def gather_kernel(
     nx, nz, n_grid,
     basis_in, panel_in,
-    coeffs_out, panel_out,
-    basis_ref, panel_ref, coeffs_ref,
+    coeffs_ref, panel_out_ref,
+    basis_ref, panel_ref,
     others, lhs, rhs, part, from_core, from_x, from_z, gathered, own,
     removed, from_band, stacked, share, pieces_of,
     gram_ref, diag, diag_right, lower, right_parts_of, projected, projected_others,
@@ -417,34 +417,32 @@
     back_z(1)
     back_core(0)
     to_x(2)
-    back_x(1)
-    to_z(2)
     hops[4].wait_recv()
     hops[5].wait_recv()
     multiply(3, (others[1, lo, :], others[1, hi, :]))
     to_core(3)
+    to_z(2)
+    to_x(3)
+    back_x(1)
+    finish(0)
     back_z(2)
-    to_x(3)
     back_core(1)
-    finish(0)
+    to_z(3)
+    back_x(2)
     finish(1)
     remove(1)
     bulks[0].start()
     bulks[1].start()
-    back_x(2)
-    to_z(3)
+    back_z(3)
     back_core(2)
+    remove(0)
     finish(2)
     remove(2)
-    back_z(3)
-    remove(0)
     back_x(3)
     back_core(3)
     for h in hops:
         h.wait_send()
     finish(3)
-    leave_coeffs = pltpu.make_async_copy(coeffs_ref, coeffs_out, io_sem.at[2])
-    leave_coeffs.start()
 
     high, low = halves(coeffs_ref[...])
     stacked[:nq, :] = high
@@ -511,7 +509,7 @@
         spread(i + 1, z)
         relay(i, order[i])
         order.append(z)
-        if i == nz // 2:
+        if i == nz // 4:
             for t in range(CORES):
                 bulks[2 + t].wait_recv()
                 removed[2, t] += from_band[1, t]
@@ -576,17 +574,14 @@
             left_parts(tile), right_parts(block, 0), preferred_element_type=jnp.float32
         )
 
-    panel_ref[...] = times(0, projected[...])
+    panel_out_ref[...] = times(0, projected[...])
     carried[2].wait_recv()
     carried[3].wait_recv()
-    panel_ref[...] += times(1, projected_others[0])
-    panel_ref[...] += times(3, projected_others[2])
+    panel_out_ref[...] += times(1, projected_others[0])
+    panel_out_ref[...] += times(3, projected_others[2])
     carried[4].wait_recv()
     carried[5].wait_recv()
-    panel_ref[...] += times(2, projected_others[1])
-    leave_panel = pltpu.make_async_copy(panel_ref, panel_out, io_sem.at[3])
-    leave_panel.start()
-    leave_coeffs.wait()
+    panel_out_ref[...] += times(2, projected_others[1])
     for h in carried:
         h.wait_send()
 
@@ -604,7 +599,6 @@
     await_bytes(pieces_of.at[0, pl.ds(0, 2)], g_send.at[2])
     await_bytes(pieces_of.at[0, 0], g_send.at[3])
     await_bytes(pieces_of.at[0], g_send.at[4])
-    leave_panel.wait()
 
 
 def reduce_and_project(nx, nz, n_grid, basis, panel):
@@ -621,12 +615,11 @@
             jax.ShapeDtypeStruct((nq, n), f32),
             jax.ShapeDtypeStruct((np_, k), f32),
         ),
-        in_specs=[pl.BlockSpec(memory_space=pl.ANY)] * 2,
-        out_specs=(pl.BlockSpec(memory_space=pl.ANY),) * 2,
+        in_specs=[pl.BlockSpec(memory_space=pltpu.HBM)] * 2,
+        out_specs=(pl.BlockSpec(memory_space=pltpu.VMEM),) * 2,
         scratch_shapes=[
             pltpu.VMEM((nq, k), f32),
             pltpu.VMEM((np_, k), f32),
-            pltpu.VMEM((nq, n), f32),
             pltpu.VMEM((BANDS - 1, np_, k), f32),
             pltpu.VMEM((nq + np_, 3 * k), jnp.bfloat16),
             pltpu.VMEM((2 * BLOCK, 3 * k), jnp.bfloat16),
@@ -660,10 +653,10 @@
             dma((3,)),
             dma((6,)),
             dma((6,)),
-            dma((4,)),
+            dma((2,)),
         ],
         compiler_params=pltpu.CompilerParams(
-            collective_id=0, has_side_effects=True, vmem_limit_bytes=60 * 1024 * 1024
+            collective_id=0, has_side_effects=True, vmem_limit_bytes=48 * 1024 * 1024
         ),
         cost_estimate=pl.CostEstimate(
             flops=60 * 1024**3, bytes_accessed=8 * 1024 * 1024, transcendentals=0

time: 152 us -> 147 us (0.967)
  Pallas kernels: 147 us -> 143 us
    pallas_call x1, Pallas kernels: 147 us -> 143 us  [reduce_and_project(): pl.pallas_call(functools.partial(gather_kernel, nx, nz, n_grid), out_shap...]
where the time goes in v5:
time: 147 us
  Pallas kernels  143 us (97%)
  local copies, waits for them, and re-layouts  3.51 us (2%)
    pallas_call x1, Pallas kernels, reduce_and_project(): pl.pallas_call(functools.partial(gather_kernel, nx, nz, n_grid), out_shap...  143 us
    unnamed x4, local copies, waits for them, and re-layouts  3.51 us

profile of v5, /device:TPU:1, one launch (start us, length us, event | category | flops | bytes accessed | tf_op | source)
XLA Modules:
  0.0 147.0 jit_solution(13309858693770939557)
XLA Ops:
  0.6 0.0 copy-start
  0.6 1.2 copy-done
  1.9 142.8 %shard_map.41 = (f32[512,1024]{1,0:T(8,128)S(1)}, f32[256,1024]{1,0:T(8,128)S(1)}) custom-call(f32[512,1024]{1,0:T(8,128)} %basis_in.1, f32[256,1024]{1,0:T(8,128)S(1)} %copy-done), custom_call_target="tpu_custom_call" | custom-call | flops 64424509440 | bytes 8388608 | tf_op jit(solution)/shard_map/pallas_call | solution.py:612
  144.7 1.0 copy.6
  145.7 1.3 copy.7
Async XLA Ops:
  0.6 1.2 copy-start

commit v6 on v5

--- a/solution.py
+++ b/solution.py
@@ -426,19 +426,19 @@
     back_x(1)
     finish(0)
     back_z(2)
+    to_z(3)
     back_core(1)
-    to_z(3)
     back_x(2)
+    back_z(3)
     finish(1)
     remove(1)
     bulks[0].start()
     bulks[1].start()
-    back_z(3)
     back_core(2)
+    back_x(3)
     remove(0)
     finish(2)
     remove(2)
-    back_x(3)
     back_core(3)
     for h in hops:
         h.wait_send()

time: 147 us -> 146 us (level)
  Pallas kernels: 143 us -> 141 us
where the time goes in v6:
time: 146 us
  Pallas kernels  141 us (97%)
  local copies, waits for them, and re-layouts  3.51 us (2%)
    pallas_call x1, Pallas kernels, reduce_and_project(): pl.pallas_call(functools.partial(gather_kernel, nx, nz, n_grid), out_shap...  141 us
    unnamed x4, local copies, waits for them, and re-layouts  3.51 us

profile of v6, /device:TPU:1, one launch (start us, length us, event | category | flops | bytes accessed | tf_op | source)
XLA Modules:
  0.0 145.5 jit_solution(12611472618341797772)
XLA Ops:
  0.6 0.0 copy-start
  0.6 1.2 copy-done
  1.9 141.4 %shard_map.41 = (f32[512,1024]{1,0:T(8,128)S(1)}, f32[256,1024]{1,0:T(8,128)S(1)}) custom-call(f32[512,1024]{1,0:T(8,128)} %basis_in.1, f32[256,1024]{1,0:T(8,128)S(1)} %copy-done), custom_call_target="tpu_custom_call" | custom-call | flops 64424509440 | bytes 8388608 | tf_op jit(solution)/shard_map/pallas_call | solution.py:612
  143.3 1.0 copy.6
  144.2 1.3 copy.7
Async XLA Ops:
  0.6 1.2 copy-start

commit v7 on v6

--- a/solution.py
+++ b/solution.py
@@ -14,7 +14,7 @@
 ROUNDS = 4
 KEPT = 3
 GROUP = 4
-EARLY = 0
+LATE = (1, 3)
 MIDWAY = 4
 ALONG_X = 4
 MESH = pl.DeviceIdType.MESH
@@ -199,7 +199,7 @@
     return done
 
 
-def factor_steps(a_ref, diag_ref, diag_right, lower_ref, right_ref, early, midway):
+def factor_steps(a_ref, diag_ref, diag_right, lower_ref, right_ref, midway):
     n = a_ref.shape[0]
     blocks = n // BLOCK
     wide = 2 * BLOCK
@@ -207,7 +207,6 @@
     right_ref[...] = jnp.zeros_like(right_ref)
 
     def step(k, carry):
-        pl.when(k == EARLY)(early)
         pl.when(k == MIDWAY)(midway)
         at = pl.ds(pl.multiple_of(k * BLOCK, BLOCK), BLOCK)
         before = pl.ds(pl.multiple_of(jnp.maximum(k - 1, 0) * BLOCK, BLOCK), BLOCK)
@@ -390,11 +389,15 @@
     bulks = [
         bulk(0, removed.at[1, 0], from_band.at[2, 0], left),
         bulk(1, removed.at[1, 1], from_band.at[0, 1], right),
-        bulk(2, removed.at[3, 0], from_band.at[1, 0], right),
-        bulk(3, removed.at[3, 1], from_band.at[1, 1], left),
-        bulk(4, removed.at[2, 0], from_band.at[0, 0], right),
-        bulk(5, removed.at[2, 1], from_band.at[2, 1], left),
     ]
+    cuts = [slice(0, BLOCK // 2), slice(BLOCK // 2, BLOCK)]
+    for i, cut in enumerate(cuts):
+        bulks += [
+            bulk(4 * i + 2, removed.at[3, 0, cut], from_band.at[1, 0, cut], right),
+            bulk(4 * i + 3, removed.at[3, 1, cut], from_band.at[1, 1, cut], left),
+            bulk(4 * i + 4, removed.at[2, 0, cut], from_band.at[0, 0, cut], right),
+            bulk(4 * i + 5, removed.at[2, 1, cut], from_band.at[2, 1, cut], left),
+        ]
 
     multiply(0, (panel_ref[lo, :], panel_ref[hi, :]))
     to_core(0)
@@ -470,8 +473,8 @@
     for _, _, device in me.over_y():
         remote(share.at[me.band], share.at[me.band], g_send.at[0], g_recv.at[0], device).start()
     remove(3)
-    bulks[2].start()
-    bulks[3].start()
+    for i in (2, 3, 6, 7):
+        bulks[i].start()
     await_bytes(share.at[pl.ds(0, BANDS - 1)], g_recv.at[0])
     pieces_of[me.core, me.x, me.z] = (share[0] + share[1]) + (share[2] + share[3])
 
@@ -509,11 +512,12 @@
         spread(i + 1, z)
         relay(i, order[i])
         order.append(z)
-        if i == nz // 4:
+        if i in LATE:
+            half_of = LATE.index(i)
             for t in range(CORES):
-                bulks[2 + t].wait_recv()
-                removed[2, t] += from_band[1, t]
-                bulks[4 + t].start()
+                bulks[4 * half_of + 2 + t].wait_recv()
+                removed[2, t, cuts[half_of]] += from_band[1, t, cuts[half_of]]
+                bulks[4 * half_of + 4 + t].start()
     cross(me.x)
     relay(nz - 1, order[nz - 1])
     cross(up)
@@ -531,9 +535,6 @@
                     to = (2 * ((band + i) % BANDS) + core) * BLOCK
                     gram_ref[to : to + BLOCK, band * np_ : (band + 1) * np_] = tile.T
 
-    await_bytes(pieces_of.at[0], g_recv.at[2])
-    place(0)
-    place(1)
     def carry(i, src, dst, device):
         return remote(src, dst, p_send.at[i], p_recv.at[i], device)
 
@@ -546,7 +547,7 @@
         carry(5, projected_others.at[0, hi], projected_others.at[1, hi], left),
     ]
     def early():
-        for i in (0, 1, 4, 5):
+        for i in (0, 1, 4, 5, 8, 9):
             bulks[i].wait_recv()
         for t in range(CORES):
             rows = slice(t * BLOCK, (t + 1) * BLOCK)
@@ -561,7 +562,11 @@
         carried[1].wait_recv()
         carried[5].start()
 
-    factor_steps(gram_ref, diag, diag_right, lower, right_parts_of, early, midway)
+    early()
+    await_bytes(pieces_of.at[0], g_recv.at[2])
+    place(0)
+    place(1)
+    factor_steps(gram_ref, diag, diag_right, lower, right_parts_of, midway)
     mine = pl.ds(pl.multiple_of(me.band * np_, np_), np_)
     row = lax.broadcasted_iota(jnp.int32, (np_, np_), 0) + me.band * np_
     col = lax.broadcasted_iota(jnp.int32, (np_, np_), 1)
@@ -645,8 +650,8 @@
             dma((6,)),
             dma((6, ROUNDS)),
             dma((6, ROUNDS)),
-            dma((6,)),
-            dma((6,)),
+            dma((10,)),
+            dma((10,)),
             dma((5,)),
             dma((nz - 1,)),
             dma((2, nz)),

time: 146 us -> 142 us (0.973)
  Pallas kernels: 141 us -> 138 us
    pallas_call x1, Pallas kernels: 141 us -> 138 us  [reduce_and_project(): pl.pallas_call(functools.partial(gather_kernel, nx, nz, n_grid), out_shap...]
where the time goes in v7:
time: 142 us
  Pallas kernels  138 us (97%)
  local copies, waits for them, and re-layouts  3.51 us (2%)
    pallas_call x1, Pallas kernels, reduce_and_project(): pl.pallas_call(functools.partial(gather_kernel, nx, nz, n_grid), out_shap...  138 us
    unnamed x4, local copies, waits for them, and re-layouts  3.51 us

profile of v7, /device:TPU:1, one launch (start us, length us, event | category | flops | bytes accessed | tf_op | source)
XLA Modules:
  0.0 141.7 jit_solution(11629245467062466900)
XLA Ops:
  0.6 0.0 copy-start
  0.6 1.2 copy-done
  1.9 137.6 %shard_map.41 = (f32[512,1024]{1,0:T(8,128)S(1)}, f32[256,1024]{1,0:T(8,128)S(1)}) custom-call(f32[512,1024]{1,0:T(8,128)} %basis_in.1, f32[256,1024]{1,0:T(8,128)S(1)} %copy-done), custom_call_target="tpu_custom_call" | custom-call | flops 64424509440 | bytes 8388608 | tf_op jit(solution)/shard_map/pallas_call | solution.py:617
  139.4 1.0 copy.6
  140.4 1.3 copy.7
Async XLA Ops:
  0.6 1.2 copy-start

commit v8 on v7

--- a/solution.py
+++ b/solution.py
@@ -522,8 +522,6 @@
     relay(nz - 1, order[nz - 1])
     cross(up)
     cross(down)
-    await_bytes(pieces_of.at[0, 0], g_recv.at[1])
-    cross(lax.rem(me.x + 2, nx))
 
     def place(core):
         for band in range(BANDS):
@@ -563,6 +561,8 @@
         carried[5].start()
 
     early()
+    await_bytes(pieces_of.at[0, 0], g_recv.at[1])
+    cross(lax.rem(me.x + 2, nx))
     await_bytes(pieces_of.at[0], g_recv.at[2])
     place(0)
     place(1)

time: 142 us -> 142 us (level)
  no operation moved by 1% of the time
where the time goes in v8:
time: 142 us
  Pallas kernels  138 us (97%)
  local copies, waits for them, and re-layouts  3.51 us (2%)
    pallas_call x1, Pallas kernels, reduce_and_project(): pl.pallas_call(functools.partial(gather_kernel, nx, nz, n_grid), out_shap...  138 us
    unnamed x4, local copies, waits for them, and re-layouts  3.51 us

profile of v8, /device:TPU:1, one launch (start us, length us, event | category | flops | bytes accessed | tf_op | source)
XLA Modules:
  0.0 141.7 jit_solution(16951941063682639980)
XLA Ops:
  0.6 0.0 copy-start
  0.6 1.2 copy-done
  1.9 137.6 %shard_map.41 = (f32[512,1024]{1,0:T(8,128)S(1)}, f32[256,1024]{1,0:T(8,128)S(1)}) custom-call(f32[512,1024]{1,0:T(8,128)} %basis_in.1, f32[256,1024]{1,0:T(8,128)S(1)} %copy-done), custom_call_target="tpu_custom_call" | custom-call | flops 64424509440 | bytes 8388608 | tf_op jit(solution)/shard_map/pallas_call | solution.py:617
  139.4 1.0 copy.6
  140.4 1.3 copy.7
Async XLA Ops:
  0.6 1.2 copy-start
